TPU v7x, 32 devices: a whole 2x2x4 slice. The times are simulated.
32 devices in a mesh: slab: 8 (over z, x), row: 4 (over y, core).
Axes of the slice: x: 2, y: 2, z: 4, core: 2. Of those that a mesh axis runs over, the one named last changes fastest.
Arguments:
- slot_brick: int32 [32, 32, 2], P(('slab', 'row')), may hold values from 0 to 255
- slot_count: int32 [32, 32, 2], P(('slab', 'row')), may hold values from 1 to 64, as said below
- point_cell: int32 [32, 32, 2, 64], P(('slab', 'row')), may hold values from 0 to 1023
- point_frac: float32 [32, 32, 2, 64], P(('slab', 'row')), may hold values from -0.5 to 0.5
- point_normal: float32 [32, 32, 2, 3, 64], P(('slab', 'row')), may hold values from -6 to 6
- point_weight: float32 [32, 32, 2, 64], P(('slab', 'row')), may hold values from 0.2 to 2
- guess: float32 [128, 64, 1024], P('slab', 'row'), may hold values from -4 to 4
Outputs:
- indicator: float32 [128, 64, 1024], P('slab', 'row')
Inputs may be any that keep to these rules, and one draw needn't show every extreme that they name: `slot_count`: every source block has at least one slot with exactly 64 live points.
All inputs are finite; a program needn't handle non-finite values.
Results may differ from a plain program's by a relative error of at most 0.0003.
Values sent between devices are 32-bit elements; how exact they have to be, the bound alone decides.
No kernel may reach another device: no remote copies, remote signals or barrier semaphores. Data moves between devices by JAX's collectives and lax.ppermute only.
A program may use at most 64 MiB of HBM per device.

v0:
```python
import functools
import jax
import jax.numpy as jnp
from jax import lax
from jax.experimental import pallas as pl
from jax.experimental.pallas import tpu as pltpu
from jax.sharding import PartitionSpec as P

Z_DEV = 16
Y_DEV = 16
NX = 1024
CAP = 64
S_PEER = 2
SWEEPS = 3
ALPHA = 4.0

HALO = 2 * SWEEPS
EXT = Z_DEV + 2 * HALO
PAIRS = EXT // 2
RIM = EXT + 2
LANES = 128
SUB = NX // LANES
CODE = 16384
UNROLL = 8
F32 = jnp.float32
BF16 = jnp.bfloat16


def chain(axis, step):
    size = lax.axis_size(axis)
    return [(i, i + step) for i in range(size) if 0 <= i + step < size]


def relax_kernel(tiles, codes, flags, guess, zlo, zhi, pay_own, pay_lo, pay_hi, out,
                 prep, acc, vr, vb, gr, gb, ir, ib, sx, st, qa, todo):
    slots = tiles * S_PEER
    halo_rows = EXT * HALO * SUB
    lane = lax.broadcasted_iota(jnp.int32, (SUB, LANES), 1)
    sub = lax.broadcasted_iota(jnp.int32, (SUB, LANES), 0)
    low = lane < CAP
    even = lane % 2 == 0
    first_lane = lane == 0
    last_lane = lane == LANES - 1
    keep_up = (sub > 0).astype(F32)
    keep_dn = (sub < SUB - 1).astype(F32)
    zero = jnp.zeros((SUB, LANES), F32)

    def parity(p):
        return even if p % 2 == 0 else jnp.logical_not(even)

    def shifts(v):
        up = jnp.where(last_lane, pltpu.roll(v, 1, 0) * keep_up, v)
        dn = jnp.where(first_lane, pltpu.roll(v, SUB - 1, 0) * keep_dn, v)
        return pltpu.roll(up, 1, 1), pltpu.roll(dn, LANES - 1, 1)

    def scan(i, pos):
        for u in range(8):
            e = codes[i * 8 + u]
            todo[pos] = e
            pos = pos + (e >= 0).astype(jnp.int32)
        return pos

    count = lax.fori_loop(0, 3 * slots // 8, scan, jnp.int32(0))
    dummy = (RIM + 1) * CODE + 3 * slots
    for u in range(UNROLL):
        todo[count + u] = jnp.int32(dummy)

    def clear(i, _):
        for u in range(12):
            acc[i * 12 + u] = zero
        return 0

    lax.fori_loop(0, 3 * RIM * RIM // 12, clear, 0)

    for block, (pay, base) in enumerate(((pay_own, 0), (pay_lo, halo_rows), (pay_hi, halo_rows))):
        def prepare(i, _, pay=pay, base=base, block=block):
            for s in range(S_PEER):
                rows = [pay[pl.ds(base + i * 64 + 2 * r + s, 8, stride=8), :] for r in range(3)]
                turned = [pltpu.roll(x, CAP, 1) for x in rows]
                cell = jnp.where(low, rows[0], turned[0])
                frac = jnp.where(low, turned[0], rows[0])
                vals = []
                for r in (1, 2):
                    vals.append(jnp.where(low, rows[r], turned[r]))
                    vals.append(jnp.where(low, turned[r], rows[r]))
                less = 0.5 - frac
                more = 0.5 + frac
                weights = (
                    jnp.where(low, 0.5 * less * less, 0.75 - frac * frac),
                    jnp.where(low, 0.5 * more * more, 0.0),
                )
                whole = cell.astype(jnp.int32)
                at = pl.multiple_of(block * slots + (i * 2 + s) * 8, 8)
                for h in range(2):
                    c = jnp.where(low, whole - 1, whole) if h == 0 else whole + 1
                    prep[16 + h, pl.ds(at, 8), :] = (c >> 7).astype(F32)
                    prep[18 + h, pl.ds(at, 8), :] = (c & 127).astype(F32)
                    for ch in range(4):
                        v = vals[ch] * weights[h]
                        head = v.astype(BF16).astype(F32)
                        prep[h * 8 + ch, pl.ds(at, 8), :] = head
                        prep[h * 8 + 4 + ch, pl.ds(at, 8), :] = v - head
            return 0

        lax.fori_loop(0, tiles // 8, prepare, 0)
    for q in range(20):
        prep[q, pl.ds(3 * slots, 8), :] = zero

    subf = sub.astype(F32)
    col = lax.broadcasted_iota(jnp.int32, (LANES, LANES), 0).astype(F32).astype(BF16)
    one = jnp.ones((LANES, LANES), BF16)
    nil = jnp.zeros((LANES, LANES), BF16)

    def splat(i, _):
        for u in range(UNROLL):
            e = todo[i * UNROLL + u]
            centre = e // CODE
            row = e % CODE
            lhs, rhs = [], []
            for h in range(2):
                hi = jnp.broadcast_to(prep[16 + h, pl.ds(row, 1), :], (SUB, LANES))
                hit = hi == subf
                parts = [
                    jnp.where(hit, jnp.broadcast_to(prep[h * 8 + q, pl.ds(row, 1), :], (SUB, LANES)), 0.0)
                    for q in range(8)
                ]
                lhs.append(jnp.concatenate(parts, axis=0))
                lo = jnp.broadcast_to(prep[18 + h, pl.ds(row, 1), :], (LANES, LANES)).astype(BF16)
                rhs.append(jnp.where(lo == col, one, nil))
            left = jnp.concatenate(lhs, axis=1).astype(BF16)
            right = jnp.concatenate(rhs, axis=1)
            res = lax.dot_general(left, right, (((1,), (1,)), ((), ())), preferred_element_type=F32)
            f = [res[ch * 8:ch * 8 + 8] + res[32 + ch * 8:40 + ch * 8] for ch in range(4)]
            size = RIM * RIM
            acc[centre] += f[0]
            acc[size + centre] += f[3]
            acc[2 * size + centre + 1] += f[1]
            acc[2 * size + centre - 1] -= f[1]
            acc[2 * size + centre + RIM] += f[2]
            acc[2 * size + centre - RIM] -= f[2]
        return 0

    lax.fori_loop(0, (count + UNROLL - 1) // UNROLL, splat, 0)

    def pack_v(z, zp, row_of):
        m = parity(zp)
        for j in range(PAIRS):
            a, b = row_of(2 * j), row_of(2 * j + 1)
            vr[z * PAIRS + j] = jnp.where(m, a, b)
            vb[z * PAIRS + j] = jnp.where(m, b, a)

    def make_rows(src, zi, z):
        def row_of(y):
            if y < HALO:
                return pay_lo[pl.ds((z * HALO + y) * SUB, SUB), :]
            if y >= HALO + Y_DEV:
                return pay_hi[pl.ds((z * HALO + y - HALO - Y_DEV) * SUB, SUB), :]
            y = y - HALO
            return src[zi, y // 8, pl.ds(y % 8, 8, stride=8), :]
        return row_of

    def pack_low(i, _):
        for u in range(2):
            pack_v(i * 2 + u, u, make_rows(zlo, i * 2 + u, i * 2 + u))
            z = HALO + Z_DEV + i * 2 + u
            pack_v(z, u, make_rows(zhi, i * 2 + u, z))
        return 0

    def pack_mid(i, _):
        for u in range(2):
            pack_v(HALO + i * 2 + u, u, make_rows(guess, i * 2 + u, HALO + i * 2 + u))
        return 0

    lax.fori_loop(0, HALO // 2, pack_low, 0)
    lax.fori_loop(0, Z_DEV // 2, pack_mid, 0)

    at_zlo, at_zhi, at_ylo, at_yhi = (flags[k] for k in range(4))

    def finish(i, _):
        for u in range(2):
            z = 1 + i * 2 + u
            m = parity(1 + u)
            fz = jnp.where(z < HALO, at_zlo, jnp.where(z >= HALO + Z_DEV, at_zhi, 1))
            size = RIM * RIM
            for j in range(PAIRS):
                fy = at_ylo if j < HALO // 2 else at_yhi if j >= (HALO + Y_DEV) // 2 else None
                f = fz if fy is None else fz * fy
                scale = jnp.broadcast_to(f.astype(F32) * (1.0 / 12.0), (SUB, LANES))
                r = (z + 1) * RIM + 2 * j + 1
                xa, xb = acc[r], acc[r + 1]
                da, db = acc[size + r], acc[size + r + 1]
                ra, rb = acc[2 * size + r], acc[2 * size + r + 1]
                xr, xbk = jnp.where(m, xa, xb), jnp.where(m, xb, xa)
                bu, bd = shifts(xbk)
                ru, rd = shifts(xr)
                gr[z * PAIRS + j] = jnp.where(m, ra, rb) + (bd - bu)
                gb[z * PAIRS + j] = jnp.where(m, rb, ra) + (rd - ru)
                ir[z * PAIRS + j] = scale / (8.0 / 3.0 + ALPHA * jnp.where(m, da, db))
                ib[z * PAIRS + j] = scale / (8.0 / 3.0 + ALPHA * jnp.where(m, db, da))
        return 0

    lax.fori_loop(0, (EXT - 2) // 2, finish, 0)

    for k in range(1, HALO + 1):
        colour = (k - 1) % 2
        vx, vy = (vr, vb) if colour == 0 else (vb, vr)
        gx, ix = (gr, ir) if colour == 0 else (gb, ib)
        j0, j1 = k // 2, PAIRS - 1 - k // 2
        wide = [j for j in range(j0 - 1, j1 + 2) if 0 <= j < PAIRS]

        def sides(p, slot, vx=vx, vy=vy, wide=wide):
            res = []
            for j in wide:
                x, y = vx[p * PAIRS + j], vy[p * PAIRS + j]
                xu, xd = shifts(x)
                yu, yd = shifts(y)
                res.append((j, xu + xd, (x + x) + (yu + yd)))
            return res

        def keep(res, slot):
            for j, s, t in res:
                sx[slot * PAIRS + j] = s
                st[slot * PAIRS + j] = t

        def advance(p, pp, slot, update, mid, colour=colour, vx=vx, gx=gx, ix=ix, j0=j0, j1=j1, wide=wide):
            m = parity(colour + pp)
            s = {j: sx[slot * PAIRS + j] for j in wide}
            t = {j: st[slot * PAIRS + j] for j in wide}
            for j in range(j0, j1 + 1):
                sl, sh = s.get(j - 1, zero), s.get(j + 1, zero)
                tl, th = t.get(j - 1, zero), t.get(j + 1, zero)
                q = (s[j] + s[j]) + t[j] + jnp.where(m, th, tl)
                if update:
                    at = (p - 1) * PAIRS + j
                    vx[at] = ix[at] * (gx[at] + (qa[PAIRS + j] + q))
                if mid:
                    d = s[j] + jnp.where(m, sl, sh)
                    qa[PAIRS + j] = (d + d) + qa[j]
                qa[j] = q

        first = k - 1
        keep(sides(first, 0), 0)
        keep(sides(first + 1, 1), 1)
        ahead = sides(first + 2, 0)
        advance(first, first, 0, False, False)
        keep(ahead, 0)
        ahead = sides(first + 3, 1)
        advance(first + 1, first + 1, 1, False, True)
        keep(ahead, 1)
        last = EXT - k

        def body(i, _, first=first, last=last):
            p = first + 2 + i * 2
            nxt0 = sides(jnp.minimum(p + 2, EXT - 1), 0)
            nxt1 = sides(jnp.minimum(p + 3, EXT - 1), 1)
            advance(p, first, 0, True, True)
            advance(p + 1, first + 1, 1, True, True)
            keep(nxt0, 0)
            keep(nxt1, 1)
            return 0

        lax.fori_loop(0, (last - first - 1) // 2, body, 0)

    def unpack(i, _):
        for u in range(2):
            z = HALO + i * 2 + u
            m = parity(u)
            for j in range(HALO // 2, (HALO + Y_DEV) // 2):
                r, b = vr[z * PAIRS + j], vb[z * PAIRS + j]
                y = 2 * j - HALO
                out[i * 2 + u, y // 8, pl.ds(y % 8, 8, stride=8), :] = jnp.where(m, r, b)
                out[i * 2 + u, y // 8, pl.ds(y % 8 + 1, 8, stride=8), :] = jnp.where(m, b, r)
        return 0

    lax.fori_loop(0, Z_DEV // 2, unpack, 0)


def as_tiles(a):
    d = a.shape[0]
    a = a.reshape(d, Y_DEV // 8, 8, SUB, LANES).transpose(0, 1, 3, 2, 4)
    return a.reshape(d, Y_DEV // 8, 8 * SUB, LANES)


def shards(slot_brick, slot_count, point_cell, point_frac, point_normal, point_weight, guess):
    n_slab, n_row = lax.axis_size("slab"), lax.axis_size("row")
    peers = point_cell.shape[1]
    tiles = 3 * peers
    slots = tiles * S_PEER

    lanes = jnp.arange(CAP, dtype=jnp.int32)
    live = (lanes < slot_count[0][:, :, None]).astype(F32)
    n = point_normal[0]
    rows0 = jnp.concatenate([point_cell[0].astype(F32), point_frac[0]], axis=-1)
    rows1 = jnp.concatenate([n[:, :, 0] * (-6.0 * live), n[:, :, 1] * (6.0 * live)], axis=-1)
    rows2 = jnp.concatenate([n[:, :, 2] * (6.0 * live), point_weight[0] * live], axis=-1)
    brick = jnp.pad((slot_brick[0] + 1).astype(F32)[:, None, :], ((0, 0), (0, 1), (0, LANES - S_PEER)))
    tile = jnp.concatenate([rows0, rows1, rows2, brick], axis=1).reshape(n_slab, n_row, 8, LANES)
    gap = jnp.zeros((1, n_row, 8, LANES), F32)
    below = jnp.concatenate([gap, tile[:-1]], axis=0)
    above = jnp.concatenate([tile[1:], gap], axis=0)
    send = jnp.stack([below, tile, above], axis=2).reshape(peers, 3, 8, LANES)

    zlo = lax.ppermute(guess[Z_DEV - HALO:], "slab", chain("slab", 1))
    zhi = lax.ppermute(guess[:HALO], "slab", chain("slab", -1))
    got = lax.all_to_all(send, ("slab", "row"), split_axis=0, concat_axis=0, tiled=True)
    points = got.reshape(tiles * 8, LANES)

    tall = jnp.concatenate([zlo, guess, zhi], axis=0)
    top = tall[:, Y_DEV - HALO:].reshape(EXT * HALO * SUB, LANES)
    bottom = tall[:, :HALO].reshape(EXT * HALO * SUB, LANES)
    pay_lo = lax.ppermute(jnp.concatenate([top, points], axis=0), "row", chain("row", 1))
    pay_hi = lax.ppermute(jnp.concatenate([bottom, points], axis=0), "row", chain("row", -1))

    halo_rows = EXT * HALO * SUB
    codes = []
    t = jnp.arange(tiles, dtype=jnp.int32)[:, None]
    s = jnp.arange(S_PEER, dtype=jnp.int32)[None, :]
    prow = ((t // 8) * 2 + s) * 8 + t % 8
    for block, (part, dy) in enumerate(((points, 0), (pay_lo[halo_rows:], -1), (pay_hi[halo_rows:], 1))):
        b = part.reshape(tiles, 8, LANES)[:, 6, :S_PEER].astype(jnp.int32) - 1
        ze = b // Y_DEV + HALO + Z_DEV * (t % 3 - 1)
        ye = b % Y_DEV + HALO + Y_DEV * dy
        inside = (b >= 0) & (ze >= 0) & (ze < EXT) & (ye >= 0) & (ye < EXT)
        entry = ((ze + 1) * RIM + ye + 1) * CODE + block * slots + prow
        codes.append(jnp.where(inside, entry, -1).reshape(-1))
    codes = jnp.concatenate(codes)
    zi, yi = lax.axis_index("slab"), lax.axis_index("row")
    flags = jnp.stack([zi > 0, zi < n_slab - 1, yi > 0, yi < n_row - 1]).astype(jnp.int32)

    vmem = pl.BlockSpec(memory_space=pltpu.VMEM)
    smem = pl.BlockSpec(memory_space=pltpu.SMEM)
    packed = pltpu.VMEM((EXT * PAIRS, SUB, LANES), F32)
    out = pl.pallas_call(
        functools.partial(relax_kernel, tiles),
        out_shape=jax.ShapeDtypeStruct((Z_DEV, Y_DEV // 8, 8 * SUB, LANES), F32),
        in_specs=[smem, smem] + [vmem] * 6,
        out_specs=vmem,
        scratch_shapes=[
            pltpu.VMEM((20, 3 * slots + 8, LANES), F32),
            pltpu.VMEM((3 * RIM * RIM, SUB, LANES), F32),
            packed, packed, packed, packed, packed, packed,
            pltpu.VMEM((2 * PAIRS, SUB, LANES), F32),
            pltpu.VMEM((2 * PAIRS, SUB, LANES), F32),
            pltpu.VMEM((2 * PAIRS, SUB, LANES), F32),
            pltpu.SMEM((3 * slots + 16,), jnp.int32),
        ],
        compiler_params=pltpu.CompilerParams(vmem_limit_bytes=60 * 1024 * 1024),
    )(codes, flags, as_tiles(guess), as_tiles(zlo), as_tiles(zhi), points, pay_lo, pay_hi)
    out = out.reshape(Z_DEV, Y_DEV // 8, SUB, 8, LANES).transpose(0, 1, 3, 2, 4)
    return out.reshape(Z_DEV, Y_DEV, NX)


def solution(mesh):
    placed = (
        P(("slab", "row"), None, None),
        P(("slab", "row"), None, None),
        P(("slab", "row"), None, None, None),
        P(("slab", "row"), None, None, None),
        P(("slab", "row"), None, None, None, None),
        P(("slab", "row"), None, None, None),
        P("slab", "row", None),
    )
    return jax.shard_map(
        shards, mesh=mesh, in_specs=placed, out_specs=P("slab", "row", None), check_vma=False
    )
```

profile of v0, /device:TPU:9, one launch (start us, length us, event | category | flops | bytes accessed | tf_op | source)
XLA Modules:
  0.0 86.1 jit_solution(15468434388853564031)
XLA Ops:
  0.0 0.0 copy-start.5
  0.0 0.0 copy-start.9
  0.0 0.0 copy-start.8
  0.0 0.0 copy-start.6
  0.0 0.0 copy-start.7
  0.0 0.0 copy-start.10
  0.0 1.3 %fusion.16 = (f32[6,16,1024]{2,1,0:T(8,128)S(1)}, f32[6,16,1024]{2,1,0:T(8,128)S(1)}) fusion(f32[16,16,1024]{2,1,0:T(8,128)} %param.13), kind=kLoop, calls=%fused_computation.70 | loop fusion | bytes 1572864 | tf_op jit(solution)/shard_map/slice | solution.py:304
  1.3 3.1 %collective-permute-start = (f32[6,16,1024]{2,1,0:T(8,128)S(1)}, f32[6,16,1024]{2,1,0:T(8,128)S(1)}, u32[]{:S(2)}, u32[]{:S(2)}) collective-permute-start(f32[6,16,1024]{2,1,0:T(8,128)S(1)} %get-tuple-element.8), channel_id=1, source_target_pairs={{0,4},{4,8},{8,12},{12,16},{16,20},{20,24},{24,28},{1,5},{5,9},{9,... | collective-permute-start | bytes 1179656 | tf_op jit(solution)/shard_map/ppermute | solution.py:303
  4.4 3.1 %collective-permute-start.1 = (f32[6,16,1024]{2,1,0:T(8,128)S(1)}, f32[6,16,1024]{2,1,0:T(8,128)S(1)}, u32[]{:S(2)}, u32[]{:S(2)}) collective-permute-start(f32[6,16,1024]{2,1,0:T(8,128)S(1)} %get-tuple-element.7), channel_id=1, source_target_pairs={{4,0},{8,4},{12,8},{16,12},{20,16},{24,20},{28,24},{5,1},{9,5},{13... | collective-permute-start | bytes 1179656 | tf_op jit(solution)/shard_map/ppermute | solution.py:304
  7.5 0.0 copy-done.5
  7.5 0.0 copy-done.9
  7.5 0.0 copy-done.8
  7.6 0.1 fusion.6
  7.6 0.1 pad_maximum_fusion.4
  7.8 0.0 copy-done.6
  7.8 0.0 copy-done.7
  7.8 0.1 pad_maximum_fusion.3
  8.0 0.0 copy-done.10
  8.0 0.1 copy.34
  8.1 0.1 fusion.14
  8.2 0.0 copy-start
  8.2 0.8 pad_maximum_fusion.2
  9.0 6.0 %all-to-all-start = ((f32[32,3,8,128]{3,2,1,0:T(8,128)}), f32[32,3,8,128]{3,2,1,0:T(8,128)S(1)}, u32[]{:S(2)}, u32[]{:S(2)}) async-start(f32[32,3,8,128]{3,2,1,0:T(8,128)} %pad_maximum_fusion.2), calls=%async_computation | async-start | bytes 786432 | tf_op jit(solution)/shard_map/all_to_all | solution.py:305
  15.0 7.9 %collective-permute-done = f32[6,16,1024]{2,1,0:T(8,128)S(1)} collective-permute-done((f32[6,16,1024]{2,1,0:T(8,128)S(1)}, f32[6,16,1024]{2,1,0:T(8,128)S(1)}, u32[]{:S(2)}, u32[]{:S(2)}) %collective-permute-start) | collective-permute-done | bytes 393248 | tf_op jit(solution)/shard_map/ppermute | solution.py:303
  22.9 0.0 copy-start.3
  22.9 0.0 copy-done
  22.9 0.1 constant_dynamic-update-slice_fusion.1
  23.0 0.6 copy-done.3
  23.6 3.0 %collective-permute-done.1 = f32[6,16,1024]{2,1,0:T(8,128)S(1)} collective-permute-done((f32[6,16,1024]{2,1,0:T(8,128)S(1)}, f32[6,16,1024]{2,1,0:T(8,128)S(1)}, u32[]{:S(2)}, u32[]{:S(2)}) %collective-permute-start.1) | collective-permute-done | bytes 393248 | tf_op jit(solution)/shard_map/ppermute | solution.py:304
  26.6 0.0 copy-start.4
  26.6 0.7 copy-done.4
  27.4 0.1 fusion.15
  27.5 0.2 reshape.171
  27.7 0.2 reshape.174
  27.9 0.9 %all-to-all-done = f32[32,3,8,128]{3,2,1,0:T(8,128)S(1)} async-done(((f32[32,3,8,128]{3,2,1,0:T(8,128)}), f32[32,3,8,128]{3,2,1,0:T(8,128)S(1)}, u32[]{:S(2)}, u32[]{:S(2)}) %all-to-all-start) | async-done | bytes 393248 | tf_op jit(solution)/shard_map/all_to_all | solution.py:305
  28.7 0.0 copy-start.1
  28.7 1.5 %pad_maximum_fusion.1 = (f32[2112,128]{1,0:T(8,128)}, f32[2112,128]{1,0:T(8,128)}) fusion(f32[768,128]{1,0:T(8,128)S(1)} %bitcast.68, f32[1344,128]{1,0:T(8,128)S(1)} %reshape.171, f32[1344,128]{1,0:T(8,128)S(1)} %reshape.174), kind=kLoop, calls=%fused_computation.1 | loop fusion | flops 540672 | bytes 3932160 | tf_op jit(solution)/shard_map/concatenate | solution.py:311
  30.2 2.9 %collective-permute-start.2 = (f32[2112,128]{1,0:T(8,128)}, f32[2112,128]{1,0:T(8,128)S(1)}, u32[]{:S(2)}, u32[]{:S(2)}) collective-permute-start(f32[2112,128]{1,0:T(8,128)} %get-tuple-element.9), channel_id=1, source_target_pairs={{0,1},{1,2},{2,3},{4,5},{5,6},{6,7},{8,9},{9,10},{10,11},{12,13},{... | collective-permute-start | bytes 3244040 | tf_op jit(solution)/shard_map/ppermute | solution.py:311
  33.1 1.9 %collective-permute-start.3 = (f32[2112,128]{1,0:T(8,128)}, f32[2112,128]{1,0:T(8,128)}, u32[]{:S(2)}, u32[]{:S(2)}) collective-permute-start(f32[2112,128]{1,0:T(8,128)} %get-tuple-element.10), channel_id=1, source_target_pairs={{1,0},{2,1},{3,2},{5,4},{6,5},{7,6},{9,8},{10,9},{11,10},{13,12},{... | collective-permute-start | bytes 3244040 | tf_op jit(solution)/shard_map/ppermute | solution.py:312
  35.1 0.1 multiply_add_fusion
  35.2 0.1 add.300
  35.3 0.1 add.286
  35.4 0.1 add.287
  35.5 0.6 add_convert_fusion.flags
  36.1 0.0 copy-done.1
  36.1 0.2 fusion.5
  36.3 0.1 sub.49
  36.4 9.1 %collective-permute-done.2.pay_lo = f32[2112,128]{1,0:T(8,128)S(1)} collective-permute-done((f32[2112,128]{1,0:T(8,128)}, f32[2112,128]{1,0:T(8,128)S(1)}, u32[]{:S(2)}, u32[]{:S(2)}) %collective-permute-start.2) | collective-permute-done | bytes 1081376 | tf_op jit(solution)/shard_map/ppermute | solution.py:311
  45.5 0.0 copy-start.2
  45.5 0.2 fusion.3
  45.7 0.1 sub.54
  45.9 4.0 %collective-permute-done.3.pay_hi = f32[2112,128]{1,0:T(8,128)} collective-permute-done((f32[2112,128]{1,0:T(8,128)}, f32[2112,128]{1,0:T(8,128)}, u32[]{:S(2)}, u32[]{:S(2)}) %collective-permute-start.3) | collective-permute-done | bytes 1081376 | tf_op jit(solution)/shard_map/ppermute | solution.py:312
  49.9 1.0 %slice_bitcast_fusion = f32[96,8,128]{2,1,0:T(8,128)S(1)} fusion(f32[2112,128]{1,0:T(8,128)} %collective-permute-done.3.pay_hi), kind=kLoop, calls=%fused_computation.2 | loop fusion | bytes 786432 | tf_op jit(solution)/shard_map/reshape | solution.py:320
  50.9 0.2 fusion.1
  51.1 0.1 sub.57
  51.3 0.7 pad_add_fusion.codes
  52.0 0.0 copy-done.2
  52.0 34.1 %shard_map.73 = f32[16,2,64,128]{3,2,1,0:T(8,128)} custom-call(s32[576]{0:T(1024)} %pad_add_fusion.codes, s32[4]{0:T(128)} %add_convert_fusion.flags, f32[16,2,64,128]{3,2,1,0:T(8,128)} %bitcast.67, f32[6,2,64,128]{3,2,1,0:T(8,128)} %bitcast.71, f32[6,2,64,128]{3,2,1,0:T(8,128)} %bitcast.72, f32[768,128]{1,0:T(8,128)} %bitcast.70, f32[2112,128]{1,0:T(8,128)} %copy-done.2, ...), custom_call_target="tpu_custom_call" | custom-call | tf_op jit(solution)/shard_map/pallas_call | solution.py:333
  (16 shorter events, 0.3 us)
Async XLA Ops:
  0.0 7.5 %copy-start.5 = (f32[1,32,2,3,64]{4,2,3,1,0:T(2,128)S(1)}, f32[1,32,2,3,64]{4,2,3,1,0:T(2,128)}, u32[]{:S(2)}) copy-start(f32[1,32,2,3,64]{4,2,3,1,0:T(2,128)} %param.11) | copy-start | bytes 147460
  0.0 7.5 %copy-start.9 = (s32[1,32,2]{1,2,0:T(2,128)S(1)}, s32[1,32,2]{1,2,0:T(2,128)}, u32[]{:S(2)}) copy-start(s32[1,32,2]{1,2,0:T(2,128)} %param.8) | copy-start | bytes 772
  0.0 7.5 %copy-start.8 = (f32[1,32,2,64]{3,2,1,0:T(2,128)S(1)}, f32[1,32,2,64]{3,2,1,0:T(2,128)}, u32[]{:S(2)}) copy-start(f32[1,32,2,64]{3,2,1,0:T(2,128)} %param.12) | copy-start | bytes 49156
  0.0 7.8 %copy-start.6 = (f32[1,32,2,64]{3,2,1,0:T(2,128)S(1)}, f32[1,32,2,64]{3,2,1,0:T(2,128)}, u32[]{:S(2)}) copy-start(f32[1,32,2,64]{3,2,1,0:T(2,128)} %param.10) | copy-start | bytes 49156
  0.0 7.8 %copy-start.7 = (s32[1,32,2,64]{3,2,1,0:T(2,128)S(1)}, s32[1,32,2,64]{3,2,1,0:T(2,128)}, u32[]{:S(2)}) copy-start(s32[1,32,2,64]{3,2,1,0:T(2,128)} %param.9) | copy-start | bytes 49156
  0.0 7.9 %copy-start.10 = (s32[1,32,2]{1,2,0:T(2,128)S(1)}, s32[1,32,2]{1,2,0:T(2,128)}, u32[]{:S(2)}) copy-start(s32[1,32,2]{1,2,0:T(2,128)} %param.7) | copy-start | bytes 772
  1.3 21.6 %collective-permute-start = (f32[6,16,1024]{2,1,0:T(8,128)S(1)}, f32[6,16,1024]{2,1,0:T(8,128)S(1)}, u32[]{:S(2)}, u32[]{:S(2)}) collective-permute-start(f32[6,16,1024]{2,1,0:T(8,128)S(1)} %get-tuple-element.8), channel_id=1, source_target_pairs={{0,4},{4,8},{8,12},{12,16},{16,20},{20,24},{24,28},{1,5},{5,9},{9,... | collective-permute-start | bytes 1179656 | tf_op jit(solution)/shard_map/ppermute | solution.py:303
  4.4 22.2 %collective-permute-start.1 = (f32[6,16,1024]{2,1,0:T(8,128)S(1)}, f32[6,16,1024]{2,1,0:T(8,128)S(1)}, u32[]{:S(2)}, u32[]{:S(2)}) collective-permute-start(f32[6,16,1024]{2,1,0:T(8,128)S(1)} %get-tuple-element.7), channel_id=1, source_target_pairs={{4,0},{8,4},{12,8},{16,12},{20,16},{24,20},{28,24},{5,1},{9,5},{13... | collective-permute-start | bytes 1179656 | tf_op jit(solution)/shard_map/ppermute | solution.py:304
  8.2 14.7 %copy-start = (f32[16,16,1024]{2,1,0:T(8,128)S(1)}, f32[16,16,1024]{2,1,0:T(8,128)}, u32[]{:S(2)}) copy-start(f32[16,16,1024]{2,1,0:T(8,128)} %param.13) | copy-start | bytes 3145732
  9.0 19.7 %all-to-all-start = ((f32[32,3,8,128]{3,2,1,0:T(8,128)}), f32[32,3,8,128]{3,2,1,0:T(8,128)S(1)}, u32[]{:S(2)}, u32[]{:S(2)}) async-start(f32[32,3,8,128]{3,2,1,0:T(8,128)} %pad_maximum_fusion.2), calls=%async_computation | async-start | bytes 786432 | tf_op jit(solution)/shard_map/all_to_all | solution.py:305
  22.9 0.7 copy-start.3
  26.6 0.7 copy-start.4
  28.7 7.4 %copy-start.1 = (f32[32,3,8,128]{3,2,1,0:T(8,128)}, f32[32,3,8,128]{3,2,1,0:T(8,128)S(1)}, u32[]{:S(2)}) copy-start(f32[32,3,8,128]{3,2,1,0:T(8,128)S(1)} %all-to-all-done) | copy-start | bytes 1179652
  30.2 15.3 %collective-permute-start.2 = (f32[2112,128]{1,0:T(8,128)}, f32[2112,128]{1,0:T(8,128)S(1)}, u32[]{:S(2)}, u32[]{:S(2)}) collective-permute-start(f32[2112,128]{1,0:T(8,128)} %get-tuple-element.9), channel_id=1, source_target_pairs={{0,1},{1,2},{2,3},{4,5},{5,6},{6,7},{8,9},{9,10},{10,11},{12,13},{... | collective-permute-start | bytes 3244040 | tf_op jit(solution)/shard_map/ppermute | solution.py:311
  33.1 16.8 %collective-permute-start.3 = (f32[2112,128]{1,0:T(8,128)}, f32[2112,128]{1,0:T(8,128)}, u32[]{:S(2)}, u32[]{:S(2)}) collective-permute-start(f32[2112,128]{1,0:T(8,128)} %get-tuple-element.10), channel_id=1, source_target_pairs={{1,0},{2,1},{3,2},{5,4},{6,5},{7,6},{9,8},{10,9},{11,10},{13,12},{... | collective-permute-start | bytes 3244040 | tf_op jit(solution)/shard_map/ppermute | solution.py:312
  45.5 6.5 %copy-start.2 = (f32[2112,128]{1,0:T(8,128)}, f32[2112,128]{1,0:T(8,128)S(1)}, u32[]{:S(2)}) copy-start(f32[2112,128]{1,0:T(8,128)S(1)} %collective-permute-done.2.pay_lo) | copy-start | bytes 3244036
where the time goes:
time: 86.2 us; the launch traced here: 86.1 us
  Pallas kernels  34.1 us (40%)
  waiting for transfers between devices  24.8 us (29%)
  starting transfers between devices  17 us (20%)
  local copies, waits for them, and re-layouts  5.28 us (6%)
  other arithmetic  4.5 us (5%)
    pallas_call x1, Pallas kernels, shards(): pl.pallas_call(functools.partial(relax_kernel, tiles), out_shape=jax.Shap...  34.1 us
    ppermute x1, waiting for transfers between devices, shards(): lax.ppermute(jnp.concatenate([top, points], axis=0), 'row', chain('row', 1))  9.08 us
    ppermute x1, waiting for transfers between devices, shards(): zlo = lax.ppermute(guess[Z_DEV - HALO:], 'slab', chain('slab', 1))  7.88 us
    all_to_all x1, starting transfers between devices, shards(): lax.all_to_all(send, ('slab', 'row'), split_axis=0, concat_axis=0, tiled=...  6.01 us
    ppermute x1, waiting for transfers between devices, shards(): lax.ppermute(jnp.concatenate([bottom, points], axis=0), 'row', chain('row...  4.04 us
    ppermute x1, starting transfers between devices, shards(): zlo = lax.ppermute(guess[Z_DEV - HALO:], 'slab', chain('slab', 1))  3.12 us
    ppermute x1, starting transfers between devices, shards(): zhi = lax.ppermute(guess[:HALO], 'slab', chain('slab', -1))  3.06 us
    ppermute x1, waiting for transfers between devices, shards(): zhi = lax.ppermute(guess[:HALO], 'slab', chain('slab', -1))  2.98 us
  transfers between devices with their start and end apart: 5, of which 5 were waited for; matrix products, arithmetic and copies ran while one was open for 4% of the time, Pallas kernels for 0%

commit v1 on v0

v1 whole, which is shorter than its diff:
```python
import functools
import jax
import jax.numpy as jnp
from jax import lax
from jax.experimental import pallas as pl
from jax.experimental.pallas import tpu as pltpu
from jax.sharding import PartitionSpec as P

Z_DEV = 16
Y_DEV = 16
NX = 1024
CAP = 64
S_PEER = 2
SWEEPS = 3
ALPHA = 4.0

HALO = 2 * SWEEPS
EXT = Z_DEV + 2 * HALO
PAIRS = EXT // 2
RIM = EXT + 2
LANES = 128
SUB = NX // LANES
CODE = 16384
UNROLL = 8
F32 = jnp.float32
BF16 = jnp.bfloat16


def chain(axis, step):
    size = lax.axis_size(axis)
    return [(i, i + step) for i in range(size) if 0 <= i + step < size]


def lane_sets():
    lane = lax.broadcasted_iota(jnp.int32, (SUB, LANES), 1)
    even = lane % 2 == 0
    return lane < CAP, (even, jnp.logical_not(even)), lane == 0, lane == LANES - 1


def find_places(pay, base, tiles, block, dy, entries):
    lane = lax.broadcasted_iota(jnp.int32, (8, LANES), 1)
    sub = lax.broadcasted_iota(jnp.int32, (8, LANES), 0)

    def find(i, _):
        brick = pay[pl.ds(base + i * 64 + 6, 8, stride=8), :].astype(jnp.int32) - 1
        t = i * 8 + sub
        dz = t - 3 * ((t * 21846) >> 16) - 1
        z = brick // Y_DEV + HALO + Z_DEV * dz
        y = brick % Y_DEV + HALO + Y_DEV * dy
        inside = (brick >= 0) & (z >= 0) & (z < EXT) & (y >= 0) & (y < EXT)
        row = block * tiles * S_PEER + (i * 2 + lane) * 8 + sub
        entry = ((z + 1) * RIM + y + 1) * CODE + row
        at = pl.multiple_of(block * tiles + i * 8, 8)
        entries[pl.ds(at, 8), :] = jnp.where(inside, entry, -1)
        return 0

    lax.fori_loop(0, tiles // 8, find, 0)


def prepare_points(pays, tiles, prep, places, todo):
    low = lane_sets()[0]
    slots = tiles * S_PEER
    group = 2
    dummy = (RIM + 1) * CODE + len(pays) * slots
    for u in range(UNROLL):
        todo[u] = jnp.int32(dummy)
    pos = jnp.int32(UNROLL)
    for block, (pay, base) in enumerate(pays):
        def prepare(i, pos, pay=pay, base=base, block=block):
            work = []
            for g in range(group):
                for s in range(S_PEER):
                    at = base + (i * group + g) * 64 + s
                    rows = [pay[pl.ds(at + 2 * r, 8, stride=8), :] for r in range(3)]
                    work.append((g, s, rows, [pltpu.roll(x, CAP, 1) for x in rows]))
            for k in range(8 * group):
                for s in range(S_PEER):
                    e = places[block * tiles + i * 8 * group + k, s]
                    todo[pos] = e
                    pos = pos + (e >= 0).astype(jnp.int32)
            for g, s, rows, turned in work:
                cell = jnp.where(low, rows[0], turned[0])
                frac = jnp.where(low, turned[0], rows[0])
                vals = []
                for r in (1, 2):
                    vals.append(jnp.where(low, rows[r], turned[r]))
                    vals.append(jnp.where(low, turned[r], rows[r]))
                less = 0.5 - frac
                more = 0.5 + frac
                weights = (
                    jnp.where(low, 0.5 * less * less, 0.75 - frac * frac),
                    jnp.where(low, 0.5 * more * more, 0.0),
                )
                whole = cell.astype(jnp.int32)
                at = pl.multiple_of(block * slots + ((i * group + g) * 2 + s) * 8, 8)
                for h in range(2):
                    c = jnp.where(low, whole - 1, whole) if h == 0 else whole + 1
                    prep[16 + h, pl.ds(at, 8), :] = (c >> 7).astype(F32)
                    prep[18 + h, pl.ds(at, 8), :] = (c & 127).astype(F32)
                    for ch in range(4):
                        v = vals[ch] * weights[h]
                        head = v.astype(BF16).astype(F32)
                        prep[h * 8 + ch, pl.ds(at, 8), :] = head
                        prep[h * 8 + 4 + ch, pl.ds(at, 8), :] = v - head
            return pos

        pos = lax.fori_loop(0, tiles // (8 * group), prepare, pos)
    zero = jnp.zeros((SUB, LANES), F32)
    for q in range(20):
        prep[q, pl.ds(len(pays) * slots, 8), :] = zero
    for u in range(UNROLL):
        todo[pos + u] = jnp.int32(dummy)
    return pos - UNROLL


def splat_slots(count, todo, prep, stage, accd, accr):
    sub = lax.broadcasted_iota(jnp.int32, (SUB, LANES), 0)
    subf = sub.astype(F32)
    keep_up = (sub > 0).astype(F32)
    keep_dn = (sub < SUB - 1).astype(F32)
    first_lane, last_lane = lane_sets()[2:]
    col = lax.broadcasted_iota(jnp.int32, (LANES, LANES), 0).astype(F32).astype(BF16)
    one = jnp.ones((LANES, LANES), BF16)
    nil = jnp.zeros((LANES, LANES), BF16)
    for q in range(4 * UNROLL):
        stage[q] = jnp.zeros((SUB, LANES), F32)

    def add(i):
        slopes = []
        for u in range(UNROLL):
            v = stage[4 * u]
            up = jnp.where(last_lane, pltpu.roll(v, 1, 0) * keep_up, v)
            dn = jnp.where(first_lane, pltpu.roll(v, SUB - 1, 0) * keep_dn, v)
            slopes.append(pltpu.roll(dn, LANES - 1, 1) - pltpu.roll(up, 1, 1))
        for u in range(UNROLL):
            centre = todo[i * UNROLL + u] // CODE
            f1, f2, f3 = (stage[4 * u + ch] for ch in range(1, 4))
            new = [
                accd[centre] + f3,
                accr[centre] + slopes[u],
                accr[centre + 1] + f1,
                accr[centre - 1] - f1,
                accr[centre + RIM] + f2,
                accr[centre - RIM] - f2,
            ]
            accd[centre] = new[0]
            accr[centre] = new[1]
            accr[centre + 1] = new[2]
            accr[centre - 1] = new[3]
            accr[centre + RIM] = new[4]
            accr[centre - RIM] = new[5]

    def splat(i, _):
        add(i)
        sums = []
        for u in range(UNROLL):
            row = todo[(i + 1) * UNROLL + u] % CODE
            lhs, rhs = [], []
            for h in range(2):
                hi = jnp.broadcast_to(prep[16 + h, pl.ds(row, 1), :], (SUB, LANES))
                hit = hi == subf
                parts = [
                    jnp.where(hit, jnp.broadcast_to(prep[h * 8 + q, pl.ds(row, 1), :], (SUB, LANES)), 0.0)
                    for q in range(8)
                ]
                lhs.append(jnp.concatenate(parts, axis=0))
                lo = jnp.broadcast_to(prep[18 + h, pl.ds(row, 1), :], (LANES, LANES)).astype(BF16)
                rhs.append(jnp.where(lo == col, one, nil))
            left = jnp.concatenate(lhs, axis=1).astype(BF16)
            right = jnp.concatenate(rhs, axis=1)
            res = lax.dot_general(left, right, (((1,), (1,)), ((), ())), preferred_element_type=F32)
            sums.append([res[ch * 8:ch * 8 + 8] + res[32 + ch * 8:40 + ch * 8] for ch in range(4)])
        for u in range(UNROLL):
            for ch in range(4):
                stage[4 * u + ch] = sums[u][ch]
        return 0

    groups = (count + UNROLL - 1) // UNROLL
    lax.fori_loop(0, groups, splat, 0)
    add(groups)


def at_row(z, j):
    return pl.ds((z * PAIRS + j) * 9 + 1, SUB)


def pack_pair(vr, vb, z, j, m, a, b):
    vr[at_row(z, j), :] = jnp.where(m, a, b)
    vb[at_row(z, j), :] = jnp.where(m, b, a)


def side_sums(v, z, pairs):
    first_lane, last_lane = lane_sets()[2:]
    res = []
    for j in pairs:
        at = (z * PAIRS + j) * 9
        x = v[pl.ds(at + 1, SUB), :]
        up = jnp.where(last_lane, v[pl.ds(at, SUB), :], x)
        dn = jnp.where(first_lane, v[pl.ds(at + 2, SUB), :], x)
        res.append((j, pltpu.roll(up, 1, 1) + pltpu.roll(dn, LANES - 1, 1)))
    return res


def keep_sums(sums, z, res):
    for j, value in res:
        sums[z * PAIRS + j] = value


def near_kernel(tiles, guess, zlo, zhi, ylo, yhi, points, accd, accr, vr, vb, sr,
                prep, stage, todo, entries, places, sem):
    zero = jnp.zeros((SUB, LANES), F32)
    par = lane_sets()[1]
    find_places(points, 0, tiles, 0, 0, entries)
    fetch = pltpu.make_async_copy(entries, places, sem.at[0])
    fetch.start()

    def clear(i, _):
        for u in range(12):
            accd[i * 12 + u] = zero
            accr[i * 12 + u] = zero
        return 0

    lax.fori_loop(0, RIM * RIM // 12, clear, 0)

    def clear_v(i, _):
        for u in range(9):
            vr[pl.ds(i * 72 + u * 8, 8), :] = zero
            vb[pl.ds(i * 72 + u * 8, 8), :] = zero
        return 0

    lax.fori_loop(0, vr.shape[0] // 72, clear_v, 0)
    fetch.wait()
    count = prepare_points(((points, 0),), tiles, prep, places, todo)
    splat_slots(count, todo, prep, stage, accd, accr)

    def edges(i, _):
        for u in range(2):
            for src, z0 in ((zlo, 0), (zhi, HALO + Z_DEV)):
                zi = i * 2 + u
                for j in range(Y_DEV // 2):
                    a = src[zi, 2 * j // 8, pl.ds(2 * j % 8, 8, stride=8), :]
                    b = src[zi, 2 * j // 8, pl.ds(2 * j % 8 + 1, 8, stride=8), :]
                    pack_pair(vr, vb, z0 + zi, HALO // 2 + j, par[u], a, b)
        return 0

    def middle(i, _):
        for u in range(2):
            zi = i * 2 + u
            for j in range(Y_DEV // 2):
                a = guess[zi, 2 * j // 8, pl.ds(2 * j % 8, 8, stride=8), :]
                b = guess[zi, 2 * j // 8, pl.ds(2 * j % 8 + 1, 8, stride=8), :]
                pack_pair(vr, vb, HALO + zi, HALO // 2 + j, par[u], a, b)
            for j in range(HALO // 2):
                y = 8 - HALO + 2 * j
                a, b = (ylo[zi, pl.ds(y + k, 8, stride=8), :] for k in range(2))
                pack_pair(vr, vb, HALO + zi, j, par[u], a, b)
                a, b = (yhi[zi, pl.ds(2 * j + k, 8, stride=8), :] for k in range(2))
                pack_pair(vr, vb, HALO + zi, (HALO + Y_DEV) // 2 + j, par[u], a, b)
        return 0

    lax.fori_loop(0, HALO // 2, edges, 0)
    lax.fori_loop(0, Z_DEV // 2, middle, 0)

    def first_sums(i, _):
        for u in range(2):
            keep_sums(sr, i * 2 + u, side_sums(vr, i * 2 + u, range(PAIRS)))
        return 0

    lax.fori_loop(0, EXT // 2, first_sums, 0)


def relax_kernel(tiles, flags, pay_lo, pay_hi, *refs):
    accd, accr, vr, vb, sr, out = refs[5:11]
    prep, stage, gr, gb, ir, ib, sb, qa, todo, entries, places, sem = refs[11:]
    par = lane_sets()[1]
    zero = jnp.zeros((SUB, LANES), F32)
    base = 2 * HALO * HALO * SUB
    pays = ((pay_lo, base), (pay_hi, base))
    find_places(pay_lo, base, tiles, 0, -1, entries)
    find_places(pay_hi, base, tiles, 1, 1, entries)
    fetch = pltpu.make_async_copy(entries, places, sem.at[0])
    fetch.start()

    edge_pairs = (*range(HALO // 2), *range((HALO + Y_DEV) // 2, PAIRS))

    def corners(i, _):
        for half in range(2):
            for u in range(2):
                zi = half * HALO + i * 2 + u
                z = zi + half * Z_DEV
                for j in range(HALO // 2):
                    for pay, j0 in ((pay_lo, 0), (pay_hi, (HALO + Y_DEV) // 2)):
                        a, b = (pay[pl.ds((zi * HALO + 2 * j + k) * SUB, SUB), :] for k in range(2))
                        pack_pair(vr, vb, z, j0 + j, par[u], a, b)
        for half in range(2):
            for u in range(2):
                z = half * (HALO + Z_DEV) + i * 2 + u
                keep_sums(sr, z, side_sums(vr, z, edge_pairs))
        return 0

    lax.fori_loop(0, HALO // 2, corners, 0)
    fetch.wait()
    count = prepare_points(pays, tiles, prep, places, todo)
    splat_slots(count, todo, prep, stage, accd, accr)

    at_zlo, at_zhi, at_ylo, at_yhi = (flags[k] for k in range(4))

    def finish(i, _):
        for u in range(2):
            z = 1 + i * 2 + u
            m = par[(1 + u) % 2]
            fz = jnp.where(z < HALO, at_zlo, jnp.where(z >= HALO + Z_DEV, at_zhi, 1))
            for j in range(PAIRS):
                fy = at_ylo if j < HALO // 2 else at_yhi if j >= (HALO + Y_DEV) // 2 else None
                f = fz if fy is None else fz * fy
                scale = jnp.broadcast_to(f.astype(F32) * (1.0 / 6.0), (SUB, LANES))
                r = (z + 1) * RIM + 2 * j + 1
                da, db = accd[r], accd[r + 1]
                ra, rb = accr[r], accr[r + 1]
                at = z * PAIRS + j
                ir[at] = scale / (8.0 / 3.0 + ALPHA * jnp.where(m, da, db))
                ib[at] = scale / (8.0 / 3.0 + ALPHA * jnp.where(m, db, da))
                gr[at] = jnp.where(m, ra, rb)
                gb[at] = jnp.where(m, rb, ra)
        return 0

    lax.fori_loop(0, (EXT - 2) // 2, finish, 0)

    def pairs_of(k):
        return [j for j in range(k // 2 - 1, PAIRS + 1 - k // 2) if 0 <= j < PAIRS]

    def arrays_of(k):
        return (vr, vb, sr, sb, gr, ir) if k % 2 else (vb, vr, sb, sr, gb, ib)

    def advance(k, p, pp, update, mid):
        vx, _, sums, others, gx, ix = arrays_of(k)
        m = par[((k - 1) % 2 + pp) % 2]
        s, t = {}, {}
        for j in pairs_of(k):
            s[j] = sums[p * PAIRS + j]
            t[j] = vx[at_row(p, j), :] + 0.5 * others[p * PAIRS + j]
        for j in range(k // 2, PAIRS - k // 2):
            q = s[j] + t[j] + jnp.where(m, t.get(j + 1, zero), t.get(j - 1, zero))
            if update:
                at = (p - 1) * PAIRS + j
                vx[at_row(p - 1, j), :] = ix[at] * (gx[at] + (qa[PAIRS + j] + q))
            if mid:
                qa[PAIRS + j] = s[j] + jnp.where(m, s.get(j - 1, zero), s.get(j + 1, zero)) + qa[j]
            qa[j] = q

    def sides(k, p):
        return side_sums(arrays_of(k)[1], p, pairs_of(k))

    def keep(k, p, res):
        keep_sums(arrays_of(k)[3], p, res)

    for p in range(2):
        keep(1, p, sides(1, p))
    for k in range(1, HALO + 1):
        first = k - 1
        ahead = [sides(k, first + 2 + u) for u in range(2)]
        advance(k, first, first, False, False)
        advance(k, first + 1, first + 1, False, True)
        for u in range(2):
            keep(k, first + 2 + u, ahead[u])
        steps = (EXT - 2 * k) // 2

        def body(i, _, k=k, first=first):
            p = first + 2 + i * 2
            ahead = [sides(k, p + 2 + u) for u in range(2)]
            advance(k, p, first, True, True)
            advance(k, p + 1, first + 1, True, True)
            for u in range(2):
                keep(k, p + 2 + u, ahead[u])
            return 0

        lax.fori_loop(0, steps - 1, body, 0)
        p = first + 2 * steps
        ahead = [sides(k + 1, k + u) for u in range(2)] if k < HALO else []
        advance(k, p, first, True, True)
        advance(k, p + 1, first + 1, True, False)
        for u, res in enumerate(ahead):
            keep(k + 1, k + u, res)

    def unpack(i, _):
        for u in range(2):
            z = HALO + i * 2 + u
            m = par[u]
            for j in range(HALO // 2, (HALO + Y_DEV) // 2):
                r, b = vr[at_row(z, j), :], vb[at_row(z, j), :]
                y = 2 * j - HALO
                out[i * 2 + u, y // 8, pl.ds(y % 8, 8, stride=8), :] = jnp.where(m, r, b)
                out[i * 2 + u, y // 8, pl.ds(y % 8 + 1, 8, stride=8), :] = jnp.where(m, b, r)
        return 0

    lax.fori_loop(0, Z_DEV // 2, unpack, 0)


def corner_kernel(zlo, zhi, points, top, bottom):
    for half, src in enumerate((zlo, zhi)):
        def corner(z, _, half=half, src=src):
            for y in range(HALO):
                at = pl.ds(((half * HALO + z) * HALO + y) * SUB, SUB)
                top[at, :] = src[z, Y_DEV // 8 - 1, pl.ds(8 - HALO + y, 8, stride=8), :]
                bottom[at, :] = src[z, 0, pl.ds(y, 8, stride=8), :]
            return 0

        lax.fori_loop(0, HALO, corner, 0)
    base = 2 * HALO * HALO * SUB

    def copy(i, _):
        for u in range(8):
            block = points[pl.ds(i * 64 + u * 8, 8), :]
            top[pl.ds(base + i * 64 + u * 8, 8), :] = block
            bottom[pl.ds(base + i * 64 + u * 8, 8), :] = block
        return 0

    lax.fori_loop(0, points.shape[0] // 64, copy, 0)


def as_tiles(a):
    d = a.shape[0]
    a = a.reshape(d, Y_DEV // 8, 8, SUB, LANES).transpose(0, 1, 3, 2, 4)
    return a.reshape(d, Y_DEV // 8, 8 * SUB, LANES)


def shards(slot_brick, slot_count, point_cell, point_frac, point_normal, point_weight, guess):
    n_slab, n_row = lax.axis_size("slab"), lax.axis_size("row")
    peers = point_cell.shape[1]
    tiles = 3 * peers
    slots = tiles * S_PEER

    lanes = jnp.arange(CAP, dtype=jnp.int32)
    live = (lanes < slot_count[0][:, :, None]).astype(F32)
    n = point_normal[0]
    rows0 = jnp.concatenate([point_cell[0].astype(F32), point_frac[0]], axis=-1)
    rows1 = jnp.concatenate([n[:, :, 0] * (-3.0 * live), n[:, :, 1] * (3.0 * live)], axis=-1)
    rows2 = jnp.concatenate([n[:, :, 2] * (3.0 * live), point_weight[0] * live], axis=-1)
    brick = jnp.pad((slot_brick[0] + 1).astype(F32)[:, None, :], ((0, 0), (0, 1), (0, LANES - S_PEER)))
    tile = jnp.concatenate([rows0, rows1, rows2, brick], axis=1).reshape(n_slab, n_row, 8, LANES)
    gap = jnp.zeros((1, n_row, 8, LANES), F32)
    below = jnp.concatenate([gap, tile[:-1]], axis=0)
    above = jnp.concatenate([tile[1:], gap], axis=0)
    send = jnp.stack([below, tile, above], axis=2).reshape(peers, 3, 8, LANES)

    zlo = lax.ppermute(guess[Z_DEV - HALO:], "slab", chain("slab", 1))
    zhi = lax.ppermute(guess[:HALO], "slab", chain("slab", -1))
    got = lax.all_to_all(send, ("slab", "row"), split_axis=0, concat_axis=0, tiled=True)
    split = as_tiles(guess)
    ylo = lax.ppermute(split[:, -1], "row", chain("row", 1))
    yhi = lax.ppermute(split[:, 0], "row", chain("row", -1))
    points = got.reshape(tiles * 8, LANES)
    zlo, zhi = as_tiles(zlo), as_tiles(zhi)

    vmem = pl.BlockSpec(memory_space=pltpu.VMEM)
    smem = pl.BlockSpec(memory_space=pltpu.SMEM)
    packed = pltpu.VMEM((EXT * PAIRS, SUB, LANES), F32)
    pay = jax.ShapeDtypeStruct((2 * HALO * HALO * SUB + tiles * 8, LANES), F32)
    top, bottom = pl.pallas_call(
        corner_kernel,
        out_shape=(pay, pay),
        in_specs=[vmem] * 3,
        out_specs=[vmem] * 2,
        compiler_params=pltpu.CompilerParams(vmem_limit_bytes=8 * 1024 * 1024),
    )(zlo, zhi, points)
    pay_lo = lax.ppermute(top, "row", chain("row", 1))
    pay_hi = lax.ppermute(bottom, "row", chain("row", -1))
    zi, yi = lax.axis_index("slab"), lax.axis_index("row")
    flags = jnp.stack([zi > 0, zi < n_slab - 1, yi > 0, yi < n_row - 1]).astype(jnp.int32)

    cells = RIM * RIM
    state = (
        jax.ShapeDtypeStruct((cells, SUB, LANES), F32),
        jax.ShapeDtypeStruct((cells, SUB, LANES), F32),
        jax.ShapeDtypeStruct(((EXT * PAIRS * 9 + 8 + 71) // 72 * 72, LANES), F32),
        jax.ShapeDtypeStruct(((EXT * PAIRS * 9 + 8 + 71) // 72 * 72, LANES), F32),
        jax.ShapeDtypeStruct((EXT * PAIRS, SUB, LANES), F32),
    )

    def lists(blocks):
        return [
            pltpu.SMEM((blocks * slots + 2 * UNROLL,), jnp.int32),
            pltpu.VMEM((blocks * tiles, LANES), jnp.int32),
            pltpu.SMEM((blocks * tiles, LANES), jnp.int32),
            pltpu.SemaphoreType.DMA((1,)),
        ]

    def limit(blocks, extra):
        return (extra << 20) + 20 * blocks * slots * LANES * 4

    held = pl.pallas_call(
        functools.partial(near_kernel, tiles),
        out_shape=state,
        in_specs=[vmem] * 6,
        out_specs=[vmem] * 5,
        scratch_shapes=[
            pltpu.VMEM((20, slots + 8, LANES), F32),
            pltpu.VMEM((4 * UNROLL, SUB, LANES), F32),
        ] + lists(1),
        cost_estimate=pl.CostEstimate(flops=40_000_000_000, bytes_accessed=1_000_000, transcendentals=0),
        compiler_params=pltpu.CompilerParams(vmem_limit_bytes=limit(1, 6)),
    )(split, zlo, zhi, ylo, yhi, points)
    out = pl.pallas_call(
        functools.partial(relax_kernel, tiles),
        out_shape=state + (jax.ShapeDtypeStruct((Z_DEV, Y_DEV // 8, 8 * SUB, LANES), F32),),
        in_specs=[smem] + [vmem] * 7,
        out_specs=[vmem] * 6,
        input_output_aliases={3 + i: i for i in range(5)},
        scratch_shapes=[
            pltpu.VMEM((20, 2 * slots + 8, LANES), F32),
            pltpu.VMEM((4 * UNROLL, SUB, LANES), F32),
            packed, packed, packed, packed, packed,
            pltpu.VMEM((2 * PAIRS, SUB, LANES), F32),
        ] + lists(2),
        compiler_params=pltpu.CompilerParams(vmem_limit_bytes=limit(2, 16)),
    )(flags, pay_lo, pay_hi, *held)[-1]
    out = out.reshape(Z_DEV, Y_DEV // 8, SUB, 8, LANES).transpose(0, 1, 3, 2, 4)
    return out.reshape(Z_DEV, Y_DEV, NX)


def solution(mesh):
    placed = (
        P(("slab", "row"), None, None),
        P(("slab", "row"), None, None),
        P(("slab", "row"), None, None, None),
        P(("slab", "row"), None, None, None),
        P(("slab", "row"), None, None, None, None),
        P(("slab", "row"), None, None, None),
        P("slab", "row", None),
    )
    return jax.shard_map(
        shards, mesh=mesh, in_specs=placed, out_specs=P("slab", "row", None), check_vma=False
    )
```

time: 86.2 us -> 75.7 us (0.88)
  the two profiles are of different devices: /device:TPU:9 before, /device:TPU:3 now
where the time goes in v1:
time: 75.7 us; the launch traced here: 75.2 us
  Pallas kernels  28.6 us (38%)
  starting transfers between devices  22.5 us (30%)
  waiting for transfers between devices  16.4 us (22%)
  local copies, waits for them, and re-layouts  4.1 us (5%)
  other arithmetic  3.37 us (4%)
    pallas_call x1, Pallas kernels, shards(): pl.pallas_call(functools.partial(relax_kernel, tiles), out_shape=state +...  19 us
    pallas_call x1, Pallas kernels, shards(): pl.pallas_call(functools.partial(near_kernel, tiles), out_shape=state, in...  9.46 us
    ppermute x1, waiting for transfers between devices, shards(): zlo = lax.ppermute(guess[Z_DEV - HALO:], 'slab', chain('slab', 1))  8.6 us
    ppermute x1, waiting for transfers between devices, shards(): zhi = lax.ppermute(guess[:HALO], 'slab', chain('slab', -1))  7.3 us
    all_to_all x1, starting transfers between devices, shards(): lax.all_to_all(send, ('slab', 'row'), split_axis=0, concat_axis=0, tiled=...  6.41 us
    ppermute x1, starting transfers between devices, shards(): zlo = lax.ppermute(guess[Z_DEV - HALO:], 'slab', chain('slab', 1))  4.16 us
    ppermute x1, starting transfers between devices, shards(): ylo = lax.ppermute(split[:, -1], 'row', chain('row', 1))  3.26 us
    ppermute x1, starting transfers between devices, shards(): pay_hi = lax.ppermute(bottom, 'row', chain('row', -1))  2.29 us
  transfers between devices with their start and end apart: 7, of which 3 were waited for; matrix products, arithmetic and copies ran while one was open for 3% of the time, Pallas kernels for 13%

profile of v1, /device:TPU:3, one launch (start us, length us, event | category | flops | bytes accessed | tf_op | source)
XLA Modules:
  0.0 75.2 jit_solution(5575182113805039051)
XLA Ops:
  0.0 0.7 convert_bitcast_fusion
  0.7 0.1 copy.45
  0.8 0.8 %fusion.1 = f32[32,2,64]{2,0,1:T(8,128)S(1)} fusion(s32[1,32,2,64]{3,2,1,0:T(2,128)} %param.9), kind=kLoop, calls=%fused_computation.19 | loop fusion | flops 4096 | bytes 32768 | tf_op jit(solution)/shard_map/convert_element_type | solution.py:436
  1.5 0.8 %copy.54 = f32[1,32,2,64]{3,1,2,0:T(8,128)S(1)} copy(f32[1,32,2,64]{3,2,1,0:T(2,128)} %param.10) | data formatting | bytes 32768 | tf_op args[3]
  2.3 0.1 pad_maximum_fusion.1
  2.4 0.0 copy-start
  2.4 1.0 %copy.53 = f32[1,32,2,3,64]{4,1,2,3,0:T(8,128)S(1)} copy(f32[1,32,2,3,64]{4,2,3,1,0:T(2,128)} %param.11) | data formatting | bytes 98304 | tf_op args[4]
  3.4 0.9 %fusion = (f32[32,2,64]{2,0,1:T(8,128)S(1)}, f32[32,2,64]{2,0,1:T(8,128)S(1)}, f32[32,2,64]{2,0,1:T(8,128)S(1)}, f32[32,2,64]{2,0,1:T(8,128)S(1)}) fusion(f32[32,2,3,64]{3,0,1,2:T(8,128)S(1)} %bitcast.81, s32[32,2]{0,1:T(2,128)} %bitcast.83, f32[1,32,2,64]{3,2,1,0:T(2,128)} %param.12), kind=kLoop, calls=%fused_computation.12 | loop fusion | flops 28672 | bytes 131328 | tf_op jit(solution)/shard_map/mul | solution.py:437
  4.3 0.1 pad_maximum_fusion.2
  4.4 0.1 fusion.2
  4.6 0.8 %pad_maximum_fusion = f32[32,3,8,128]{3,2,1,0:T(8,128)} fusion(f32[32,1,8,128]{3,2,1,0:T(8,128)S(1)} %bitcast.77, f32[32,1,8,128]{3,2,1,0:T(8,128)S(1)} %get-tuple-element.27, f32[32,1,8,128]{3,2,1,0:T(8,128)S(1)} %bitcast.78), kind=kLoop, calls=%fused_computation.3 | loop fusion | flops 196608 | bytes 786432 | tf_op jit(solution)/shard_map/stack | solution.py:444
  5.3 6.4 %all-to-all-start = ((f32[32,3,8,128]{3,2,1,0:T(8,128)}), f32[32,3,8,128]{3,2,1,0:T(8,128)S(1)}, u32[]{:S(2)}, u32[]{:S(2)}) async-start(f32[32,3,8,128]{3,2,1,0:T(8,128)} %pad_maximum_fusion), calls=%async_computation | async-start | bytes 786432 | tf_op jit(solution)/shard_map/all_to_all | solution.py:448
  11.7 0.0 copy-done
  11.8 0.1 copy_bitcast_fusion
  11.8 1.1 %slice_bitcast_fusion = (f32[16,64,128]{2,1,0:T(8,128)}, f32[16,64,128]{2,1,0:T(8,128)}) fusion(f32[16,2,64,128]{3,2,0,1:T(8,128)S(1)} %copy_bitcast_fusion), kind=kLoop, calls=%fused_computation.1 | loop fusion | bytes 2097152 | tf_op jit(solution)/shard_map/squeeze | solution.py:451
  12.9 2.3 %collective-permute-start.5 = (f32[16,64,128]{2,1,0:T(8,128)}, f32[16,64,128]{2,1,0:T(8,128)S(1)}, u32[]{:S(2)}, u32[]{:S(2)}) collective-permute-start(f32[16,64,128]{2,1,0:T(8,128)} %get-tuple-element.21), channel_id=1, source_target_pairs={{1,0},{2,1},{3,2},{5,4},{6,5},{7,6},{9,8},{10,9},{11,10},{13,12},{... | collective-permute-start | bytes 1572872 | tf_op jit(solution)/shard_map/ppermute | solution.py:451
  15.2 3.3 %collective-permute-start.4 = (f32[16,64,128]{2,1,0:T(8,128)}, f32[16,64,128]{2,1,0:T(8,128)S(1)}, u32[]{:S(2)}, u32[]{:S(2)}) collective-permute-start(f32[16,64,128]{2,1,0:T(8,128)} %get-tuple-element.22), channel_id=1, source_target_pairs={{0,1},{1,2},{2,3},{4,5},{5,6},{6,7},{8,9},{9,10},{10,11},{12,13},{... | collective-permute-start | bytes 1572872 | tf_op jit(solution)/shard_map/ppermute | solution.py:450
  18.5 1.0 %fusion.3 = (f32[6,16,1024]{2,1,0:T(8,128)}, f32[6,16,1024]{2,1,0:T(8,128)}) fusion(f32[16,16,1024]{2,1,0:T(8,128)S(1)} %copy-done), kind=kLoop, calls=%fused_computation.24 | loop fusion | bytes 1572864 | tf_op jit(solution)/shard_map/slice | solution.py:447
  19.5 2.0 %collective-permute-start.1 = (f32[6,16,1024]{2,1,0:T(8,128)}, f32[6,16,1024]{2,1,0:T(8,128)S(1)}, u32[]{:S(2)}, u32[]{:S(2)}) collective-permute-start(f32[6,16,1024]{2,1,0:T(8,128)} %get-tuple-element.23), channel_id=1, source_target_pairs={{4,0},{8,4},{12,8},{16,12},{20,16},{24,20},{28,24},{5,1},{9,5},{13... | collective-permute-start | bytes 1179656 | tf_op jit(solution)/shard_map/ppermute | solution.py:447
  21.5 4.2 %collective-permute-start = (f32[6,16,1024]{2,1,0:T(8,128)}, f32[6,16,1024]{2,1,0:T(8,128)S(1)}, u32[]{:S(2)}, u32[]{:S(2)}) collective-permute-start(f32[6,16,1024]{2,1,0:T(8,128)} %get-tuple-element.24), channel_id=1, source_target_pairs={{0,4},{4,8},{8,12},{12,16},{16,20},{20,24},{24,28},{1,5},{5,9},{9,... | collective-permute-start | bytes 1179656 | tf_op jit(solution)/shard_map/ppermute | solution.py:446
  25.7 0.1 add_convert_fusion.flags
  25.7 7.3 %collective-permute-done.1 = f32[6,16,1024]{2,1,0:T(8,128)S(1)} collective-permute-done((f32[6,16,1024]{2,1,0:T(8,128)}, f32[6,16,1024]{2,1,0:T(8,128)S(1)}, u32[]{:S(2)}, u32[]{:S(2)}) %collective-permute-start.1) | collective-permute-done | bytes 393248 | tf_op jit(solution)/shard_map/ppermute | solution.py:447
  33.0 8.6 %collective-permute-done = f32[6,16,1024]{2,1,0:T(8,128)S(1)} collective-permute-done((f32[6,16,1024]{2,1,0:T(8,128)}, f32[6,16,1024]{2,1,0:T(8,128)S(1)}, u32[]{:S(2)}, u32[]{:S(2)}) %collective-permute-start) | collective-permute-done | bytes 393248 | tf_op jit(solution)/shard_map/ppermute | solution.py:446
  41.6 0.0 all-to-all-done
  41.6 0.2 shard_map.73
  41.9 2.1 %collective-permute-start.2 = (f32[1344,128]{1,0:T(8,128)S(1)}, f32[1344,128]{1,0:T(8,128)S(1)}, u32[]{:S(2)}, u32[]{:S(2)}) collective-permute-start(f32[1344,128]{1,0:T(8,128)S(1)} %get-tuple-element.13), channel_id=1, source_target_pairs={{0,1},{1,2},{2,3},{4,5},{5,6},{6,7},{8,9},{9,10},{10,11},{12,13},{... | collective-permute-start | bytes 2064392 | tf_op jit(solution)/shard_map/ppermute | solution.py:466
  43.9 2.3 %collective-permute-start.3 = (f32[1344,128]{1,0:T(8,128)S(1)}, f32[1344,128]{1,0:T(8,128)S(1)}, u32[]{:S(2)}, u32[]{:S(2)}) collective-permute-start(f32[1344,128]{1,0:T(8,128)S(1)} %get-tuple-element.14), channel_id=1, source_target_pairs={{1,0},{2,1},{3,2},{5,4},{6,5},{7,6},{9,8},{10,9},{11,10},{13,12},{... | collective-permute-start | bytes 2064392 | tf_op jit(solution)/shard_map/ppermute | solution.py:467
  46.2 0.0 collective-permute-done.5.yhi
  46.2 0.0 collective-permute-done.4.ylo
  46.3 9.5 %shard_map.74 = (f32[900,8,128]{2,1,0:T(8,128)S(1)}, f32[900,8,128]{2,1,0:T(8,128)S(1)}, f32[3600,128]{1,0:T(8,128)S(1)}, f32[3600,128]{1,0:T(8,128)S(1)}, f32[392,8,128]{2,1,0:T(8,128)S(1)}) custom-call(f32[16,2,64,128]{3,2,1,0:T(8,128)S(1)} %bitcast.70, f32[6,2,64,128]{3,2,1,0:T(8,128)S(1)} %bitcast.76, f32[6,2,64,128]{3,2,1,0:T(8,128)S(1)} %bitcast.74, ...), custom_call_target="tpu_custom_call" | custom-call | flops 40000000000 | bytes 1000000 | tf_op jit(solution)/shard_map/pallas_call | solution.py:491
  55.7 0.0 collective-permute-done.2.pay_lo
  55.7 0.5 collective-permute-done.3.pay_hi
  56.2 19.0 %shard_map.75 = (f32[900,8,128]{2,1,0:T(8,128)S(1)}, f32[900,8,128]{2,1,0:T(8,128)S(1)}, f32[3600,128]{1,0:T(8,128)S(1)}, f32[3600,128]{1,0:T(8,128)S(1)}, f32[3...) custom-call(s32[4]{0:T(128)S(1)} %add_convert_fusion.flags, ...), custom_call_target="tpu_custom_call", output_to_operand_aliasing={{0}: (3, {}), {1}: (4, {}), {2}: (5, {}), {3}: (6, {}), {4}... | custom-call | tf_op jit(solution)/shard_map/pallas_call | solution.py:503
  (6 shorter events, 0.1 us)
Async XLA Ops:
  2.4 9.3 %copy-start = (f32[16,16,1024]{2,1,0:T(8,128)S(1)}, f32[16,16,1024]{2,1,0:T(8,128)}, u32[]{:S(2)}) copy-start(f32[16,16,1024]{2,1,0:T(8,128)} %param.13) | copy-start | bytes 3145732
  5.3 36.3 %all-to-all-start = ((f32[32,3,8,128]{3,2,1,0:T(8,128)}), f32[32,3,8,128]{3,2,1,0:T(8,128)S(1)}, u32[]{:S(2)}, u32[]{:S(2)}) async-start(f32[32,3,8,128]{3,2,1,0:T(8,128)} %pad_maximum_fusion), calls=%async_computation | async-start | bytes 786432 | tf_op jit(solution)/shard_map/all_to_all | solution.py:448
  12.9 33.3 %collective-permute-start.5 = (f32[16,64,128]{2,1,0:T(8,128)}, f32[16,64,128]{2,1,0:T(8,128)S(1)}, u32[]{:S(2)}, u32[]{:S(2)}) collective-permute-start(f32[16,64,128]{2,1,0:T(8,128)} %get-tuple-element.21), channel_id=1, source_target_pairs={{1,0},{2,1},{3,2},{5,4},{6,5},{7,6},{9,8},{10,9},{11,10},{13,12},{... | collective-permute-start | bytes 1572872 | tf_op jit(solution)/shard_map/ppermute | solution.py:451
  15.2 31.0 %collective-permute-start.4 = (f32[16,64,128]{2,1,0:T(8,128)}, f32[16,64,128]{2,1,0:T(8,128)S(1)}, u32[]{:S(2)}, u32[]{:S(2)}) collective-permute-start(f32[16,64,128]{2,1,0:T(8,128)} %get-tuple-element.22), channel_id=1, source_target_pairs={{0,1},{1,2},{2,3},{4,5},{5,6},{6,7},{8,9},{9,10},{10,11},{12,13},{... | collective-permute-start | bytes 1572872 | tf_op jit(solution)/shard_map/ppermute | solution.py:450
  19.5 13.6 %collective-permute-start.1 = (f32[6,16,1024]{2,1,0:T(8,128)}, f32[6,16,1024]{2,1,0:T(8,128)S(1)}, u32[]{:S(2)}, u32[]{:S(2)}) collective-permute-start(f32[6,16,1024]{2,1,0:T(8,128)} %get-tuple-element.23), channel_id=1, source_target_pairs={{4,0},{8,4},{12,8},{16,12},{20,16},{24,20},{28,24},{5,1},{9,5},{13... | collective-permute-start | bytes 1179656 | tf_op jit(solution)/shard_map/ppermute | solution.py:447
  21.5 20.2 %collective-permute-start = (f32[6,16,1024]{2,1,0:T(8,128)}, f32[6,16,1024]{2,1,0:T(8,128)S(1)}, u32[]{:S(2)}, u32[]{:S(2)}) collective-permute-start(f32[6,16,1024]{2,1,0:T(8,128)} %get-tuple-element.24), channel_id=1, source_target_pairs={{0,4},{4,8},{8,12},{12,16},{16,20},{20,24},{24,28},{1,5},{5,9},{9,... | collective-permute-start | bytes 1179656 | tf_op jit(solution)/shard_map/ppermute | solution.py:446
  41.9 13.9 %collective-permute-start.2 = (f32[1344,128]{1,0:T(8,128)S(1)}, f32[1344,128]{1,0:T(8,128)S(1)}, u32[]{:S(2)}, u32[]{:S(2)}) collective-permute-start(f32[1344,128]{1,0:T(8,128)S(1)} %get-tuple-element.13), channel_id=1, source_target_pairs={{0,1},{1,2},{2,3},{4,5},{5,6},{6,7},{8,9},{9,10},{10,11},{12,13},{... | collective-permute-start | bytes 2064392 | tf_op jit(solution)/shard_map/ppermute | solution.py:466
  43.9 12.3 %collective-permute-start.3 = (f32[1344,128]{1,0:T(8,128)S(1)}, f32[1344,128]{1,0:T(8,128)S(1)}, u32[]{:S(2)}, u32[]{:S(2)}) collective-permute-start(f32[1344,128]{1,0:T(8,128)S(1)} %get-tuple-element.14), channel_id=1, source_target_pairs={{1,0},{2,1},{3,2},{5,4},{6,5},{7,6},{9,8},{10,9},{11,10},{13,12},{... | collective-permute-start | bytes 2064392 | tf_op jit(solution)/shard_map/ppermute | solution.py:467

commit v2 on v1

--- a/solution.py
+++ b/solution.py
@@ -21,7 +21,7 @@
 LANES = 128
 SUB = NX // LANES
 CODE = 16384
-UNROLL = 8
+UNROLL = 16
 F32 = jnp.float32
 BF16 = jnp.bfloat16
 
@@ -29,6 +29,11 @@
 def chain(axis, step):
     size = lax.axis_size(axis)
     return [(i, i + step) for i in range(size) if 0 <= i + step < size]
+
+
+def swaps(axis, start):
+    pairs = [(i, i + 1) for i in range(start, lax.axis_size(axis) - 1, 2)]
+    return pairs + [(j, i) for i, j in pairs]
 
 
 def lane_sets():
@@ -73,11 +78,13 @@
                     at = base + (i * group + g) * 64 + s
                     rows = [pay[pl.ds(at + 2 * r, 8, stride=8), :] for r in range(3)]
                     work.append((g, s, rows, [pltpu.roll(x, CAP, 1) for x in rows]))
-            for k in range(8 * group):
-                for s in range(S_PEER):
-                    e = places[block * tiles + i * 8 * group + k, s]
+            for half in range(group):
+                found = [
+                    places[block * tiles + (i * group + half) * 8 + k, s] for k in range(8) for s in range(S_PEER)
+                ]
+                for e in found:
                     todo[pos] = e
-                    pos = pos + (e >= 0).astype(jnp.int32)
+                    pos = pos + (1 + (e >> 31))
             for g, s, rows, turned in work:
                 cell = jnp.where(low, rows[0], turned[0])
                 frac = jnp.where(low, turned[0], rows[0])
@@ -133,7 +140,7 @@
             dn = jnp.where(first_lane, pltpu.roll(v, SUB - 1, 0) * keep_dn, v)
             slopes.append(pltpu.roll(dn, LANES - 1, 1) - pltpu.roll(up, 1, 1))
         for u in range(UNROLL):
-            centre = todo[i * UNROLL + u] // CODE
+            centre = todo[i * UNROLL + u] >> 14
             f1, f2, f3 = (stage[4 * u + ch] for ch in range(1, 4))
             new = [
                 accd[centre] + f3,
@@ -154,7 +161,7 @@
         add(i)
         sums = []
         for u in range(UNROLL):
-            row = todo[(i + 1) * UNROLL + u] % CODE
+            row = todo[(i + 1) * UNROLL + u] & (CODE - 1)
             lhs, rhs = [], []
             for h in range(2):
                 hi = jnp.broadcast_to(prep[16 + h, pl.ds(row, 1), :], (SUB, LANES))
@@ -206,6 +213,64 @@
         sums[z * PAIRS + j] = value
 
 
+def deal_kernel(n_row, brick_in, number_in, guess, cell_in, frac_in, normal_in, weight_in, send, low_planes, high_planes,
+                brick, number, cell, frac, normal, weight, sem):
+    moves = [
+        pltpu.make_async_copy(guess.at[pl.ds(0, HALO)], low_planes, sem.at[0]),
+        pltpu.make_async_copy(guess.at[pl.ds(Z_DEV - HALO, HALO)], high_planes, sem.at[1]),
+    ]
+    pairs = ((brick_in, brick), (number_in, number), (cell_in, cell), (frac_in, frac), (normal_in, normal),
+             (weight_in, weight))
+    loads = [pltpu.make_async_copy(src, dst, sem.at[2 + i]) for i, (src, dst) in enumerate(pairs)]
+    for move in loads + moves:
+        move.start()
+    peers = cell.shape[0]
+    lane = lax.broadcasted_iota(jnp.int32, (S_PEER, CAP), 1)
+    sub = lax.broadcasted_iota(jnp.int32, (S_PEER, CAP), 0)
+    wide = lax.broadcasted_iota(jnp.int32, (2, LANES), 1)
+    top = lax.broadcasted_iota(jnp.int32, (2, LANES), 0) == 0
+    empty = jnp.zeros((8, LANES), F32)
+    for d in range(n_row):
+        send[d, 0] = empty
+        send[peers - 1 - d, 2] = empty
+    for move in loads:
+        move.wait()
+    group = 4
+
+    def tile(i, _):
+        for g in range(group):
+            d = i * group + g
+            live = (lane < jnp.where(sub == 0, number[0, d], number[1, d])).astype(F32)
+            first = brick[0, d] + 1
+            second = brick[1, d] + 1
+            place = jnp.where(wide == 0, first, jnp.where(wide == 1, second, 0))
+            place = jnp.where(top, place, 0).astype(F32)
+            pieces = (
+                jnp.concatenate([cell[d].astype(F32), frac[d]], axis=1),
+                jnp.concatenate([normal[d, 0] * (-3.0 * live), normal[d, 1] * (3.0 * live)], axis=1),
+                jnp.concatenate([normal[d, 2] * (3.0 * live), weight[d] * live], axis=1),
+                place,
+            )
+            for r, piece in enumerate(pieces):
+                send[d, 1, 2 * r:2 * r + 2, :] = piece
+        return 0
+
+    lax.fori_loop(0, peers // group, tile, 0)
+
+    def spread(i, _):
+        for g in range(group):
+            d = i * group + g
+            block = send[d, 1]
+            below = send[d + n_row, 1]
+            send[d + n_row, 0] = block
+            send[d, 2] = below
+        return 0
+
+    lax.fori_loop(0, (peers - n_row) // group, spread, 0)
+    for move in moves:
+        move.wait()
+
+
 def near_kernel(tiles, guess, zlo, zhi, ylo, yhi, points, accd, accr, vr, vb, sr,
                 prep, stage, todo, entries, places, sem):
     zero = jnp.zeros((SUB, LANES), F32)
@@ -229,9 +294,6 @@
         return 0
 
     lax.fori_loop(0, vr.shape[0] // 72, clear_v, 0)
-    fetch.wait()
-    count = prepare_points(((points, 0),), tiles, prep, places, todo)
-    splat_slots(count, todo, prep, stage, accd, accr)
 
     def edges(i, _):
         for u in range(2):
@@ -262,22 +324,29 @@
     lax.fori_loop(0, Z_DEV // 2, middle, 0)
 
     def first_sums(i, _):
-        for u in range(2):
-            keep_sums(sr, i * 2 + u, side_sums(vr, i * 2 + u, range(PAIRS)))
-        return 0
-
-    lax.fori_loop(0, EXT // 2, first_sums, 0)
-
-
-def relax_kernel(tiles, flags, pay_lo, pay_hi, *refs):
+        res = [side_sums(vr, i * 4 + u, range(PAIRS)) for u in range(4)]
+        for u in range(4):
+            keep_sums(sr, i * 4 + u, res[u])
+        return 0
+
+    lax.fori_loop(0, EXT // 4, first_sums, 0)
+    fetch.wait()
+    count = prepare_points(((points, 0),), tiles, prep, places, todo)
+    splat_slots(count, todo, prep, stage, accd, accr)
+
+
+def relax_kernel(tiles, flags, pay_outer, pay_inner, *refs):
     accd, accr, vr, vb, sr, out = refs[5:11]
-    prep, stage, gr, gb, ir, ib, sb, qa, todo, entries, places, sem = refs[11:]
+    prep, stage, gr, gb, ir, ib, sb, qa, held, out_sem, todo, entries, places, sem = refs[11:]
     par = lane_sets()[1]
     zero = jnp.zeros((SUB, LANES), F32)
     base = 2 * HALO * HALO * SUB
-    pays = ((pay_lo, base), (pay_hi, base))
-    find_places(pay_lo, base, tiles, 0, -1, entries)
-    find_places(pay_hi, base, tiles, 1, 1, entries)
+    pays = ((pay_outer, base), (pay_inner, base))
+    at_zlo, at_zhi, at_ylo, at_yhi, odd = (flags[k] for k in range(5))
+    side = 2 * odd - 1
+    find_places(pay_outer, base, tiles, 0, side, entries)
+    find_places(pay_inner, base, tiles, 1, -side, entries)
+    high = (HALO + Y_DEV) // 2
     fetch = pltpu.make_async_copy(entries, places, sem.at[0])
     fetch.start()
 
@@ -289,7 +358,7 @@
                 zi = half * HALO + i * 2 + u
                 z = zi + half * Z_DEV
                 for j in range(HALO // 2):
-                    for pay, j0 in ((pay_lo, 0), (pay_hi, (HALO + Y_DEV) // 2)):
+                    for pay, j0 in ((pay_outer, high * odd), (pay_inner, high * (1 - odd))):
                         a, b = (pay[pl.ds((zi * HALO + 2 * j + k) * SUB, SUB), :] for k in range(2))
                         pack_pair(vr, vb, z, j0 + j, par[u], a, b)
         for half in range(2):
@@ -302,8 +371,6 @@
     fetch.wait()
     count = prepare_points(pays, tiles, prep, places, todo)
     splat_slots(count, todo, prep, stage, accd, accr)
-
-    at_zlo, at_zhi, at_ylo, at_yhi = (flags[k] for k in range(4))
 
     def finish(i, _):
         for u in range(2):
@@ -354,6 +421,19 @@
     def keep(k, p, res):
         keep_sums(arrays_of(k)[3], p, res)
 
+    def leave(z):
+        return pltpu.make_async_copy(held.at[pl.ds(z, 2)], out.at[pl.ds(z, 2)], out_sem.at[z // 2])
+
+    def unpack(z):
+        for u in range(2):
+            m = par[u]
+            for j in range(HALO // 2, (HALO + Y_DEV) // 2):
+                r, b = vr[at_row(HALO + z + u, j), :], vb[at_row(HALO + z + u, j), :]
+                y = 2 * j - HALO
+                held[z + u, y // 8, pl.ds(y % 8, 8, stride=8), :] = jnp.where(m, r, b)
+                held[z + u, y // 8, pl.ds(y % 8 + 1, 8, stride=8), :] = jnp.where(m, b, r)
+        leave(z).start()
+
     for p in range(2):
         keep(1, p, sides(1, p))
     for k in range(1, HALO + 1):
@@ -365,44 +445,55 @@
             keep(k, first + 2 + u, ahead[u])
         steps = (EXT - 2 * k) // 2
 
-        def body(i, _, k=k, first=first):
-            p = first + 2 + i * 2
-            ahead = [sides(k, p + 2 + u) for u in range(2)]
+        def body(p, k=k, first=first, n=2):
+            ahead = [sides(k, p + n + u) for u in range(n)]
+            for u in range(n):
+                advance(k, p + u, first + u, True, True)
+            for u in range(n):
+                keep(k, p + n + u, ahead[u])
+
+        def body4(i, _, k=k, first=first, body=body):
+            p = first + 2 + i * 4
+            ahead = [sides(k, p + 2 + u) for u in range(4)]
             advance(k, p, first, True, True)
             advance(k, p + 1, first + 1, True, True)
-            for u in range(2):
+            for u in range(4):
                 keep(k, p + 2 + u, ahead[u])
+            advance(k, p + 2, first, True, True)
+            advance(k, p + 3, first + 1, True, True)
+            if k == HALO:
+                unpack(i * 4)
+                unpack(i * 4 + 2)
             return 0
 
-        lax.fori_loop(0, steps - 1, body, 0)
+        lax.fori_loop(0, (steps - 1) // 2, body4, 0)
+        if (steps - 1) % 2:
+            body(first + 2 + (steps - 2) * 2)
+            if k == HALO:
+                unpack((steps - 2) * 2)
         p = first + 2 * steps
         ahead = [sides(k + 1, k + u) for u in range(2)] if k < HALO else []
         advance(k, p, first, True, True)
         advance(k, p + 1, first + 1, True, False)
         for u, res in enumerate(ahead):
             keep(k + 1, k + u, res)
-
-    def unpack(i, _):
-        for u in range(2):
-            z = HALO + i * 2 + u
-            m = par[u]
-            for j in range(HALO // 2, (HALO + Y_DEV) // 2):
-                r, b = vr[at_row(z, j), :], vb[at_row(z, j), :]
-                y = 2 * j - HALO
-                out[i * 2 + u, y // 8, pl.ds(y % 8, 8, stride=8), :] = jnp.where(m, r, b)
-                out[i * 2 + u, y // 8, pl.ds(y % 8 + 1, 8, stride=8), :] = jnp.where(m, b, r)
-        return 0
-
-    lax.fori_loop(0, Z_DEV // 2, unpack, 0)
-
-
-def corner_kernel(zlo, zhi, points, top, bottom):
+        if k == HALO:
+            unpack((steps - 1) * 2)
+
+    for z in range(0, Z_DEV, 2):
+        leave(z).wait()
+
+
+def corner_kernel(odd_ref, zlo, zhi, points, outer, inner):
+    odd = odd_ref[0]
+    ends = [(Y_DEV // 8 - 1) * side for side in (odd, 1 - odd)]
+    starts = [(8 - HALO) * side for side in (odd, 1 - odd)]
     for half, src in enumerate((zlo, zhi)):
         def corner(z, _, half=half, src=src):
             for y in range(HALO):
                 at = pl.ds(((half * HALO + z) * HALO + y) * SUB, SUB)
-                top[at, :] = src[z, Y_DEV // 8 - 1, pl.ds(8 - HALO + y, 8, stride=8), :]
-                bottom[at, :] = src[z, 0, pl.ds(y, 8, stride=8), :]
+                outer[at, :] = src[z, ends[0], pl.ds(starts[0] + y, 8, stride=8), :]
+                inner[at, :] = src[z, ends[1], pl.ds(starts[1] + y, 8, stride=8), :]
             return 0
 
         lax.fori_loop(0, HALO, corner, 0)
@@ -411,8 +502,8 @@
     def copy(i, _):
         for u in range(8):
             block = points[pl.ds(i * 64 + u * 8, 8), :]
-            top[pl.ds(base + i * 64 + u * 8, 8), :] = block
-            bottom[pl.ds(base + i * 64 + u * 8, 8), :] = block
+            outer[pl.ds(base + i * 64 + u * 8, 8), :] = block
+            inner[pl.ds(base + i * 64 + u * 8, 8), :] = block
         return 0
 
     lax.fori_loop(0, points.shape[0] // 64, copy, 0)
@@ -430,43 +521,31 @@
     tiles = 3 * peers
     slots = tiles * S_PEER
 
-    lanes = jnp.arange(CAP, dtype=jnp.int32)
-    live = (lanes < slot_count[0][:, :, None]).astype(F32)
-    n = point_normal[0]
-    rows0 = jnp.concatenate([point_cell[0].astype(F32), point_frac[0]], axis=-1)
-    rows1 = jnp.concatenate([n[:, :, 0] * (-3.0 * live), n[:, :, 1] * (3.0 * live)], axis=-1)
-    rows2 = jnp.concatenate([n[:, :, 2] * (3.0 * live), point_weight[0] * live], axis=-1)
-    brick = jnp.pad((slot_brick[0] + 1).astype(F32)[:, None, :], ((0, 0), (0, 1), (0, LANES - S_PEER)))
-    tile = jnp.concatenate([rows0, rows1, rows2, brick], axis=1).reshape(n_slab, n_row, 8, LANES)
-    gap = jnp.zeros((1, n_row, 8, LANES), F32)
-    below = jnp.concatenate([gap, tile[:-1]], axis=0)
-    above = jnp.concatenate([tile[1:], gap], axis=0)
-    send = jnp.stack([below, tile, above], axis=2).reshape(peers, 3, 8, LANES)
-
-    zlo = lax.ppermute(guess[Z_DEV - HALO:], "slab", chain("slab", 1))
-    zhi = lax.ppermute(guess[:HALO], "slab", chain("slab", -1))
-    got = lax.all_to_all(send, ("slab", "row"), split_axis=0, concat_axis=0, tiled=True)
-    split = as_tiles(guess)
-    ylo = lax.ppermute(split[:, -1], "row", chain("row", 1))
-    yhi = lax.ppermute(split[:, 0], "row", chain("row", -1))
-    points = got.reshape(tiles * 8, LANES)
-    zlo, zhi = as_tiles(zlo), as_tiles(zhi)
-
     vmem = pl.BlockSpec(memory_space=pltpu.VMEM)
     smem = pl.BlockSpec(memory_space=pltpu.SMEM)
-    packed = pltpu.VMEM((EXT * PAIRS, SUB, LANES), F32)
-    pay = jax.ShapeDtypeStruct((2 * HALO * HALO * SUB + tiles * 8, LANES), F32)
-    top, bottom = pl.pallas_call(
-        corner_kernel,
-        out_shape=(pay, pay),
-        in_specs=[vmem] * 3,
-        out_specs=[vmem] * 2,
-        compiler_params=pltpu.CompilerParams(vmem_limit_bytes=8 * 1024 * 1024),
-    )(zlo, zhi, points)
-    pay_lo = lax.ppermute(top, "row", chain("row", 1))
-    pay_hi = lax.ppermute(bottom, "row", chain("row", -1))
-    zi, yi = lax.axis_index("slab"), lax.axis_index("row")
-    flags = jnp.stack([zi > 0, zi < n_slab - 1, yi > 0, yi < n_row - 1]).astype(jnp.int32)
+    hbm = pl.BlockSpec(memory_space=pltpu.HBM)
+    small = pltpu.CompilerParams(vmem_limit_bytes=8 * 1024 * 1024)
+    split = as_tiles(guess)
+    planes = jax.ShapeDtypeStruct((HALO,) + split.shape[1:], F32)
+    send, low_planes, high_planes = pl.pallas_call(
+        functools.partial(deal_kernel, n_row),
+        out_shape=(jax.ShapeDtypeStruct((peers, 3, 8, LANES), F32), planes, planes),
+        in_specs=[hbm] * 7,
+        out_specs=[vmem] * 3,
+        scratch_shapes=[
+            pltpu.SMEM((S_PEER, peers), jnp.int32),
+            pltpu.SMEM((S_PEER, peers), jnp.int32),
+            pltpu.VMEM((peers, S_PEER, CAP), jnp.int32),
+            pltpu.VMEM((peers, S_PEER, CAP), F32),
+            pltpu.VMEM((peers, 3, S_PEER, CAP), F32),
+            pltpu.VMEM((peers, S_PEER, CAP), F32),
+            pltpu.SemaphoreType.DMA((8,)),
+        ],
+        compiler_params=pltpu.CompilerParams(vmem_limit_bytes=60 * 1024 * 1024),
+    )(
+        slot_brick[0].T, slot_count[0].T, split, point_cell[0], point_frac[0],
+        jnp.transpose(point_normal[0], (0, 2, 1, 3)), point_weight[0],
+    )
 
     cells = RIM * RIM
     state = (
@@ -476,6 +555,26 @@
         jax.ShapeDtypeStruct(((EXT * PAIRS * 9 + 8 + 71) // 72 * 72, LANES), F32),
         jax.ShapeDtypeStruct((EXT * PAIRS, SUB, LANES), F32),
     )
+    zlo = lax.ppermute(high_planes, "slab", chain("slab", 1))
+    zhi = lax.ppermute(low_planes, "slab", chain("slab", -1))
+    got = lax.all_to_all(send, ("slab", "row"), split_axis=0, concat_axis=0, tiled=True)
+    ylo = lax.ppermute(split[:, -1], "row", chain("row", 1))
+    yhi = lax.ppermute(split[:, 0], "row", chain("row", -1))
+    points = got.reshape(tiles * 8, LANES)
+
+    packed = pltpu.VMEM((EXT * PAIRS, SUB, LANES), F32)
+    pay = jax.ShapeDtypeStruct((2 * HALO * HALO * SUB + tiles * 8, LANES), F32)
+    zi, yi = lax.axis_index("slab"), lax.axis_index("row")
+    flags = jnp.stack([zi > 0, zi < n_slab - 1, yi > 0, yi < n_row - 1, yi % 2 == 1]).astype(jnp.int32)
+    outer, inner = pl.pallas_call(
+        corner_kernel,
+        out_shape=(pay, pay),
+        in_specs=[smem] + [vmem] * 3,
+        out_specs=[vmem] * 2,
+        compiler_params=small,
+    )(flags[4:], zlo, zhi, points)
+    pay_outer = lax.ppermute(outer, "row", swaps("row", 1))
+    pay_inner = lax.ppermute(inner, "row", swaps("row", 0))
 
     def lists(blocks):
         return [
@@ -504,16 +603,18 @@
         functools.partial(relax_kernel, tiles),
         out_shape=state + (jax.ShapeDtypeStruct((Z_DEV, Y_DEV // 8, 8 * SUB, LANES), F32),),
         in_specs=[smem] + [vmem] * 7,
-        out_specs=[vmem] * 6,
+        out_specs=[vmem] * 5 + [hbm],
         input_output_aliases={3 + i: i for i in range(5)},
         scratch_shapes=[
             pltpu.VMEM((20, 2 * slots + 8, LANES), F32),
             pltpu.VMEM((4 * UNROLL, SUB, LANES), F32),
             packed, packed, packed, packed, packed,
             pltpu.VMEM((2 * PAIRS, SUB, LANES), F32),
+            pltpu.VMEM((Z_DEV, Y_DEV // 8, 8 * SUB, LANES), F32),
+            pltpu.SemaphoreType.DMA((Z_DEV // 2,)),
         ] + lists(2),
-        compiler_params=pltpu.CompilerParams(vmem_limit_bytes=limit(2, 16)),
-    )(flags, pay_lo, pay_hi, *held)[-1]
+        compiler_params=pltpu.CompilerParams(vmem_limit_bytes=limit(2, 18)),
+    )(flags, pay_outer, pay_inner, *held)[-1]
     out = out.reshape(Z_DEV, Y_DEV // 8, SUB, 8, LANES).transpose(0, 1, 3, 2, 4)
     return out.reshape(Z_DEV, Y_DEV, NX)
 

time: 75.7 us -> 68 us (0.90)
  the two profiles are of different devices: /device:TPU:3 before, /device:TPU:9 now
where the time goes in v2:
time: 68 us; the launch traced here: 67.4 us
  Pallas kernels  27.7 us (41%)
  starting transfers between devices  20.2 us (30%)
  waiting for transfers between devices  17.4 us (26%)
  local copies, waits for them, and re-layouts  1.89 us (3%)
    pallas_call x1, Pallas kernels, shards(): pl.pallas_call(functools.partial(relax_kernel, tiles), out_shape=state +...  16.1 us
    ppermute x1, waiting for transfers between devices, shards(): zlo = lax.ppermute(high_planes, 'slab', chain('slab', 1))  13.5 us
    pallas_call x1, Pallas kernels, shards(): pl.pallas_call(functools.partial(near_kernel, tiles), out_shape=state, in...  7.96 us
    all_to_all x1, starting transfers between devices, shards(): lax.all_to_all(send, ('slab', 'row'), split_axis=0, concat_axis=0, tiled=...  6.33 us
    ppermute x1, starting transfers between devices, shards(): ylo = lax.ppermute(split[:, -1], 'row', chain('row', 1))  3.26 us
    ppermute x1, starting transfers between devices, shards(): zlo = lax.ppermute(high_planes, 'slab', chain('slab', 1))  3.09 us
    ppermute x1, starting transfers between devices, shards(): zhi = lax.ppermute(low_planes, 'slab', chain('slab', -1))  3.09 us
    pallas_call x1, Pallas kernels, shards(): pl.pallas_call(functools.partial(deal_kernel, n_row), out_shape=(jax.Shap...  2.86 us
  transfers between devices with their start and end apart: 7, of which 3 were waited for; matrix products, arithmetic and copies ran while one was open for 3% of the time, Pallas kernels for 13%

profile of v2, /device:TPU:9, one launch (start us, length us, event | category | flops | bytes accessed | tf_op | source)
XLA Modules:
  0.0 67.4 jit_solution(15872009702683236076)
XLA Ops:
  0.0 0.0 copy-start
  0.0 2.9 %shard_map.73 = (f32[32,3,8,128]{3,2,1,0:T(8,128)}, f32[6,2,64,128]{3,2,1,0:T(8,128)}, f32[6,2,64,128]{3,2,1,0:T(8,128)}) custom-call(s32[2,32]{1,0:T(2,128)} %bitcast.44, s32[2,32]{1,0:T(2,128)} %bitcast.45, f32[16,2,64,128]{3,2,1,0:T(8,128)} %bitcast.36, s32[32,2,64]{2,1,0:T(2,128)} %bitcast.41, f32[32,2,64]{2,1,0:T(2,128)} %bitcast.42, ...), custom_call_target="tpu_custom_call" | custom-call | tf_op jit(solution)/shard_map/pallas_call | solution.py:530
  2.9 6.3 %all-to-all-start = ((f32[32,3,8,128]{3,2,1,0:T(8,128)}), f32[32,3,8,128]{3,2,1,0:T(8,128)S(1)}, u32[]{:S(2)}, u32[]{:S(2)}) async-start(f32[32,3,8,128]{3,2,1,0:T(8,128)} %get-tuple-element.18), calls=%async_computation | async-start | bytes 786432 | tf_op jit(solution)/shard_map/all_to_all | solution.py:560
  9.2 0.0 copy-done
  9.2 0.1 copy_bitcast_fusion
  9.3 1.1 %slice_bitcast_fusion = (f32[16,64,128]{2,1,0:T(8,128)}, f32[16,64,128]{2,1,0:T(8,128)}) fusion(f32[16,2,64,128]{3,2,0,1:T(8,128)S(1)} %copy_bitcast_fusion), kind=kLoop, calls=%fused_computation.1 | loop fusion | bytes 2097152 | tf_op jit(solution)/shard_map/squeeze | solution.py:562
  10.4 2.3 %collective-permute-start.5 = (f32[16,64,128]{2,1,0:T(8,128)}, f32[16,64,128]{2,1,0:T(8,128)S(1)}, u32[]{:S(2)}, u32[]{:S(2)}) collective-permute-start(f32[16,64,128]{2,1,0:T(8,128)} %get-tuple-element.27), channel_id=1, source_target_pairs={{1,0},{2,1},{3,2},{5,4},{6,5},{7,6},{9,8},{10,9},{11,10},{13,12},{... | collective-permute-start | bytes 1572872 | tf_op jit(solution)/shard_map/ppermute | solution.py:562
  12.7 3.3 %collective-permute-start.4 = (f32[16,64,128]{2,1,0:T(8,128)}, f32[16,64,128]{2,1,0:T(8,128)S(1)}, u32[]{:S(2)}, u32[]{:S(2)}) collective-permute-start(f32[16,64,128]{2,1,0:T(8,128)} %get-tuple-element.28), channel_id=1, source_target_pairs={{0,1},{1,2},{2,3},{4,5},{5,6},{6,7},{8,9},{9,10},{10,11},{12,13},{... | collective-permute-start | bytes 1572872 | tf_op jit(solution)/shard_map/ppermute | solution.py:561
  16.0 3.1 %collective-permute-start = (f32[6,2,64,128]{3,2,1,0:T(8,128)}, f32[6,2,64,128]{3,2,1,0:T(8,128)S(1)}, u32[]{:S(2)}, u32[]{:S(2)}) collective-permute-start(f32[6,2,64,128]{3,2,1,0:T(8,128)} %get-tuple-element.16), channel_id=1, source_target_pairs={{0,4},{4,8},{8,12},{12,16},{16,20},{20,24},{24,28},{1,5},{5,9},{9,... | collective-permute-start | bytes 1179656 | tf_op jit(solution)/shard_map/ppermute | solution.py:558
  19.1 3.1 %collective-permute-start.1 = (f32[6,2,64,128]{3,2,1,0:T(8,128)}, f32[6,2,64,128]{3,2,1,0:T(8,128)S(1)}, u32[]{:S(2)}, u32[]{:S(2)}) collective-permute-start(f32[6,2,64,128]{3,2,1,0:T(8,128)} %get-tuple-element.17), channel_id=1, source_target_pairs={{4,0},{8,4},{12,8},{16,12},{20,16},{24,20},{28,24},{5,1},{9,5},{13... | collective-permute-start | bytes 1179656 | tf_op jit(solution)/shard_map/ppermute | solution.py:559
  22.2 0.1 stack.23
  22.3 0.6 slice.9.odd_ref
  22.9 13.5 %collective-permute-done.zlo = f32[6,2,64,128]{3,2,1,0:T(8,128)S(1)} collective-permute-done((f32[6,2,64,128]{3,2,1,0:T(8,128)}, f32[6,2,64,128]{3,2,1,0:T(8,128)S(1)}, u32[]{:S(2)}, u32[]{:S(2)}) %collective-permute-start) | collective-permute-done | bytes 393248 | tf_op jit(solution)/shard_map/ppermute | solution.py:558
  36.4 1.8 %collective-permute-done.1.zhi = f32[6,2,64,128]{3,2,1,0:T(8,128)S(1)} collective-permute-done((f32[6,2,64,128]{3,2,1,0:T(8,128)}, f32[6,2,64,128]{3,2,1,0:T(8,128)S(1)}, u32[]{:S(2)}, u32[]{:S(2)}) %collective-permute-start.1) | collective-permute-done | bytes 393248 | tf_op jit(solution)/shard_map/ppermute | solution.py:559
  38.2 0.0 all-to-all-done
  38.2 0.8 %shard_map.74 = (f32[1344,128]{1,0:T(8,128)S(1)}, f32[1344,128]{1,0:T(8,128)S(1)}) custom-call(s32[1]{0:T(128)} %slice.9.odd_ref, f32[6,2,64,128]{3,2,1,0:T(8,128)S(1)} %collective-permute-done.zlo, f32[6,2,64,128]{3,2,1,0:T(8,128)S(1)} %collective-permute-done.1.zhi, f32[768,128]{1,0:T(8,128)S(1)} %bitcast.38), custom_call_target="tpu_custom_call" | custom-call | tf_op jit(solution)/shard_map/pallas_call | solution.py:569
  39.0 2.1 %collective-permute-start.2 = (f32[1344,128]{1,0:T(8,128)S(1)}, f32[1344,128]{1,0:T(8,128)S(1)}, u32[]{:S(2)}, u32[]{:S(2)}) collective-permute-start(f32[1344,128]{1,0:T(8,128)S(1)} %get-tuple-element.19), channel_id=1, source_target_pairs={{1,2},{2,1},{5,6},{6,5},{9,10},{10,9},{13,14},{14,13},{17,18},{18,... | collective-permute-start | bytes 2064392 | tf_op jit(solution)/shard_map/ppermute | solution.py:576
  41.1 0.1 collective-permute-start.3
  41.2 0.0 collective-permute-done.5.yhi
  41.2 0.0 collective-permute-done.4.ylo
  41.2 8.0 %shard_map.75 = (f32[900,8,128]{2,1,0:T(8,128)S(1)}, f32[900,8,128]{2,1,0:T(8,128)S(1)}, f32[3600,128]{1,0:T(8,128)S(1)}, f32[3600,128]{1,0:T(8,128)S(1)}, f32[392,8,128]{2,1,0:T(8,128)S(1)}) custom-call(f32[16,2,64,128]{3,2,1,0:T(8,128)S(1)} %bitcast.37, f32[6,2,64,128]{3,2,1,0:T(8,128)S(1)} %collective-permute-done.zlo, ...), custom_call_target="tpu_custom_call" | custom-call | flops 40000000000 | bytes 1000000 | tf_op jit(solution)/shard_map/pallas_call | solution.py:590
  49.2 2.1 %collective-permute-done.2.pay_outer = f32[1344,128]{1,0:T(8,128)S(1)} collective-permute-done((f32[1344,128]{1,0:T(8,128)S(1)}, f32[1344,128]{1,0:T(8,128)S(1)}, u32[]{:S(2)}, u32[]{:S(2)}) %collective-permute-start.2) | collective-permute-done | bytes 688160 | tf_op jit(solution)/shard_map/ppermute | solution.py:576
  51.3 0.0 collective-permute-done.3.pay_inner
  51.3 16.1 %shard_map.76 = (f32[900,8,128]{2,1,0:T(8,128)S(1)}, f32[900,8,128]{2,1,0:T(8,128)S(1)}, f32[3600,128]{1,0:T(8,128)S(1)}, f32[3600,128]{1,0:T(8,128)S(1)}, f32[3...) custom-call(s32[5]{0:T(128)S(1)} %convert_element_type.3.flags, ...), custom_call_target="tpu_custom_call", output_to_operand_aliasing={{0}: (3, {}), {1}: (4, {}), {2}: (5, {}), {3}: (6, {}), {4}... | custom-call | tf_op jit(solution)/shard_map/pallas_call | solution.py:602
  (1 shorter events, 0.0 us)
Async XLA Ops:
  0.0 9.2 %copy-start = (f32[16,16,1024]{2,1,0:T(8,128)S(1)}, f32[16,16,1024]{2,1,0:T(8,128)}, u32[]{:S(2)}) copy-start(f32[16,16,1024]{2,1,0:T(8,128)} %param.13) | copy-start | bytes 3145732
  2.9 35.3 %all-to-all-start = ((f32[32,3,8,128]{3,2,1,0:T(8,128)}), f32[32,3,8,128]{3,2,1,0:T(8,128)S(1)}, u32[]{:S(2)}, u32[]{:S(2)}) async-start(f32[32,3,8,128]{3,2,1,0:T(8,128)} %get-tuple-element.18), calls=%async_computation | async-start | bytes 786432 | tf_op jit(solution)/shard_map/all_to_all | solution.py:560
  10.4 30.8 %collective-permute-start.5 = (f32[16,64,128]{2,1,0:T(8,128)}, f32[16,64,128]{2,1,0:T(8,128)S(1)}, u32[]{:S(2)}, u32[]{:S(2)}) collective-permute-start(f32[16,64,128]{2,1,0:T(8,128)} %get-tuple-element.27), channel_id=1, source_target_pairs={{1,0},{2,1},{3,2},{5,4},{6,5},{7,6},{9,8},{10,9},{11,10},{13,12},{... | collective-permute-start | bytes 1572872 | tf_op jit(solution)/shard_map/ppermute | solution.py:562
  12.7 28.5 %collective-permute-start.4 = (f32[16,64,128]{2,1,0:T(8,128)}, f32[16,64,128]{2,1,0:T(8,128)S(1)}, u32[]{:S(2)}, u32[]{:S(2)}) collective-permute-start(f32[16,64,128]{2,1,0:T(8,128)} %get-tuple-element.28), channel_id=1, source_target_pairs={{0,1},{1,2},{2,3},{4,5},{5,6},{6,7},{8,9},{9,10},{10,11},{12,13},{... | collective-permute-start | bytes 1572872 | tf_op jit(solution)/shard_map/ppermute | solution.py:561
  16.0 20.4 %collective-permute-start = (f32[6,2,64,128]{3,2,1,0:T(8,128)}, f32[6,2,64,128]{3,2,1,0:T(8,128)S(1)}, u32[]{:S(2)}, u32[]{:S(2)}) collective-permute-start(f32[6,2,64,128]{3,2,1,0:T(8,128)} %get-tuple-element.16), channel_id=1, source_target_pairs={{0,4},{4,8},{8,12},{12,16},{16,20},{20,24},{24,28},{1,5},{5,9},{9,... | collective-permute-start | bytes 1179656 | tf_op jit(solution)/shard_map/ppermute | solution.py:558
  19.1 19.1 %collective-permute-start.1 = (f32[6,2,64,128]{3,2,1,0:T(8,128)}, f32[6,2,64,128]{3,2,1,0:T(8,128)S(1)}, u32[]{:S(2)}, u32[]{:S(2)}) collective-permute-start(f32[6,2,64,128]{3,2,1,0:T(8,128)} %get-tuple-element.17), channel_id=1, source_target_pairs={{4,0},{8,4},{12,8},{16,12},{20,16},{24,20},{28,24},{5,1},{9,5},{13... | collective-permute-start | bytes 1179656 | tf_op jit(solution)/shard_map/ppermute | solution.py:559
  39.0 12.3 %collective-permute-start.2 = (f32[1344,128]{1,0:T(8,128)S(1)}, f32[1344,128]{1,0:T(8,128)S(1)}, u32[]{:S(2)}, u32[]{:S(2)}) collective-permute-start(f32[1344,128]{1,0:T(8,128)S(1)} %get-tuple-element.19), channel_id=1, source_target_pairs={{1,2},{2,1},{5,6},{6,5},{9,10},{10,9},{13,14},{14,13},{17,18},{18,... | collective-permute-start | bytes 2064392 | tf_op jit(solution)/shard_map/ppermute | solution.py:576
  41.1 10.2 %collective-permute-start.3 = (f32[1344,128]{1,0:T(8,128)S(1)}, f32[1344,128]{1,0:T(8,128)S(1)}, u32[]{:S(2)}, u32[]{:S(2)}) collective-permute-start(f32[1344,128]{1,0:T(8,128)S(1)} %get-tuple-element.20), channel_id=1, source_target_pairs={{0,1},{2,3},{1,0},{3,2},{4,5},{6,7},{5,4},{7,6},{8,9},{10,11},{9,8... | collective-permute-start | bytes 2064392 | tf_op jit(solution)/shard_map/ppermute | solution.py:577

commit v3 on v2

--- a/solution.py
+++ b/solution.py
@@ -42,30 +42,42 @@
     return lane < CAP, (even, jnp.logical_not(even)), lane == 0, lane == LANES - 1
 
 
-def find_places(pay, base, tiles, block, dy, entries):
+def brick_rows(pay, tiles):
+    peers = tiles // 3
+    parts = max(1, S_PEER * peers // LANES)
+    found = []
+    for which in range(3):
+        for part in range(parts):
+            total = jnp.zeros((8, LANES), F32)
+            for i in range(peers // 8):
+                total = total + pay[pl.ds(i * 192 + which * 8 + 6 + part, 8, stride=24), :]
+            found.append(jnp.sum(total, axis=0, keepdims=True))
+    found.append(jnp.zeros((8 - len(found), LANES), F32))
+    return jnp.concatenate(found, axis=0)
+
+
+def find_places(bricks, tiles, block, dy, entries):
+    parts = max(1, S_PEER * tiles // 3 // LANES)
     lane = lax.broadcasted_iota(jnp.int32, (8, LANES), 1)
     sub = lax.broadcasted_iota(jnp.int32, (8, LANES), 0)
-
-    def find(i, _):
-        brick = pay[pl.ds(base + i * 64 + 6, 8, stride=8), :].astype(jnp.int32) - 1
-        t = i * 8 + sub
-        dz = t - 3 * ((t * 21846) >> 16) - 1
-        z = brick // Y_DEV + HALO + Z_DEV * dz
-        y = brick % Y_DEV + HALO + Y_DEV * dy
-        inside = (brick >= 0) & (z >= 0) & (z < EXT) & (y >= 0) & (y < EXT)
-        row = block * tiles * S_PEER + (i * 2 + lane) * 8 + sub
-        entry = ((z + 1) * RIM + y + 1) * CODE + row
-        at = pl.multiple_of(block * tiles + i * 8, 8)
-        entries[pl.ds(at, 8), :] = jnp.where(inside, entry, -1)
-        return 0
-
-    lax.fori_loop(0, tiles // 8, find, 0)
-
-
-def prepare_points(pays, tiles, prep, places, todo):
+    brick = bricks.astype(jnp.int32) - 1
+    if parts == 1:
+        which, at = sub, lane
+    else:
+        which, at = sub >> 1, ((sub & 1) << 7) + lane
+    t = (at >> 1) * 3 + which
+    z = (brick >> 4) + HALO + Z_DEV * (which - 1)
+    y = (brick & (Y_DEV - 1)) + HALO + Y_DEV * dy
+    inside = (brick >= 0) & (z >= 0) & (z < EXT) & (y >= 0) & (y < EXT)
+    row = block * tiles * S_PEER + (((t >> 3) * 2 + (at & 1)) << 3) + (t & 7)
+    entries[pl.ds(block * 8, 8), :] = jnp.where(inside, ((z + 1) * RIM + y + 1) * CODE + row, -1)
+
+
+def prepare_points(pays, tiles, step, prep, places, todo):
     low = lane_sets()[0]
     slots = tiles * S_PEER
-    group = 2
+    width = min(LANES, S_PEER * tiles // 3)
+    group = width // (8 * S_PEER)
     dummy = (RIM + 1) * CODE + len(pays) * slots
     for u in range(UNROLL):
         todo[u] = jnp.int32(dummy)
@@ -75,13 +87,11 @@
             work = []
             for g in range(group):
                 for s in range(S_PEER):
-                    at = base + (i * group + g) * 64 + s
-                    rows = [pay[pl.ds(at + 2 * r, 8, stride=8), :] for r in range(3)]
+                    at = base + (i * group + g) * (8 * step) + s
+                    rows = [pay[pl.ds(at + 2 * r, 8, stride=step), :] for r in range(3)]
                     work.append((g, s, rows, [pltpu.roll(x, CAP, 1) for x in rows]))
-            for half in range(group):
-                found = [
-                    places[block * tiles + (i * group + half) * 8 + k, s] for k in range(8) for s in range(S_PEER)
-                ]
+            for c in range(0, width, 8):
+                found = [places[block * 8 + i, c + k] for k in range(8)]
                 for e in found:
                     todo[pos] = e
                     pos = pos + (1 + (e >> 31))
@@ -213,43 +223,59 @@
         sums[z * PAIRS + j] = value
 
 
-def deal_kernel(n_row, brick_in, number_in, guess, cell_in, frac_in, normal_in, weight_in, send, low_planes, high_planes,
+def slab_kernel(guess, outer, inner, held, sem_in, sem_out):
+    odd = lax.axis_index("slab") % 2
+    far = Z_DEV - HALO
+    half = HALO // 2
+    into, out = [], []
+    for i, (first, dst) in enumerate(((far * odd, outer), (far * (1 - odd), inner))):
+        for k in range(2):
+            n = i * 2 + k
+            into.append(pltpu.make_async_copy(guess.at[pl.ds(first + k * half, half)], held.at[n], sem_in.at[n]))
+            out.append(pltpu.make_async_copy(held.at[n], dst.at[pl.ds(k * half, half)], sem_out.at[n]))
+    for move in into:
+        move.start()
+    for first, second in zip(into, out):
+        first.wait()
+        second.start()
+    for move in out:
+        move.wait()
+
+
+def deal_kernel(n_row, brick_in, number_in, cell_in, frac_in, normal_in, weight_in, send,
                 brick, number, cell, frac, normal, weight, sem):
-    moves = [
-        pltpu.make_async_copy(guess.at[pl.ds(0, HALO)], low_planes, sem.at[0]),
-        pltpu.make_async_copy(guess.at[pl.ds(Z_DEV - HALO, HALO)], high_planes, sem.at[1]),
+    loads = [
+        pltpu.make_async_copy(src, dst, sem.at[i])
+        for i, (src, dst) in enumerate((
+            (brick_in, brick), (number_in, number), (cell_in, cell), (frac_in, frac), (normal_in, normal),
+            (weight_in, weight),
+        ))
     ]
-    pairs = ((brick_in, brick), (number_in, number), (cell_in, cell), (frac_in, frac), (normal_in, normal),
-             (weight_in, weight))
-    loads = [pltpu.make_async_copy(src, dst, sem.at[2 + i]) for i, (src, dst) in enumerate(pairs)]
-    for move in loads + moves:
-        move.start()
+    for load in loads:
+        load.start()
     peers = cell.shape[0]
     lane = lax.broadcasted_iota(jnp.int32, (S_PEER, CAP), 1)
     sub = lax.broadcasted_iota(jnp.int32, (S_PEER, CAP), 0)
-    wide = lax.broadcasted_iota(jnp.int32, (2, LANES), 1)
-    top = lax.broadcasted_iota(jnp.int32, (2, LANES), 0) == 0
+    mine = (lax.axis_index("slab") * n_row + lax.axis_index("row")) * S_PEER
+    wide = lax.broadcasted_iota(jnp.int32, (2, LANES), 1) + LANES * lax.broadcasted_iota(jnp.int32, (2, LANES), 0)
     empty = jnp.zeros((8, LANES), F32)
     for d in range(n_row):
         send[d, 0] = empty
         send[peers - 1 - d, 2] = empty
-    for move in loads:
-        move.wait()
     group = 4
+    for load in loads:
+        load.wait()
 
     def tile(i, _):
         for g in range(group):
             d = i * group + g
             live = (lane < jnp.where(sub == 0, number[0, d], number[1, d])).astype(F32)
-            first = brick[0, d] + 1
-            second = brick[1, d] + 1
-            place = jnp.where(wide == 0, first, jnp.where(wide == 1, second, 0))
-            place = jnp.where(top, place, 0).astype(F32)
+            place = jnp.where(wide == mine, brick[0, d] + 1, jnp.where(wide == mine + 1, brick[1, d] + 1, 0))
             pieces = (
                 jnp.concatenate([cell[d].astype(F32), frac[d]], axis=1),
                 jnp.concatenate([normal[d, 0] * (-3.0 * live), normal[d, 1] * (3.0 * live)], axis=1),
                 jnp.concatenate([normal[d, 2] * (3.0 * live), weight[d] * live], axis=1),
-                place,
+                place.astype(F32),
             )
             for r, piece in enumerate(pieces):
                 send[d, 1, 2 * r:2 * r + 2, :] = piece
@@ -267,15 +293,15 @@
         return 0
 
     lax.fori_loop(0, (peers - n_row) // group, spread, 0)
-    for move in moves:
-        move.wait()
-
-
-def near_kernel(tiles, guess, zlo, zhi, ylo, yhi, points, accd, accr, vr, vb, sr,
+
+
+def near_kernel(tiles, guess, z_outer, z_inner, ylo, yhi, points, accd, accr, vr, vb, sr,
                 prep, stage, todo, entries, places, sem):
     zero = jnp.zeros((SUB, LANES), F32)
     par = lane_sets()[1]
-    find_places(points, 0, tiles, 0, 0, entries)
+    odd_slab = lax.axis_index("slab") % 2
+    high = HALO + Z_DEV
+    find_places(brick_rows(points, tiles), tiles, 0, 0, entries)
     fetch = pltpu.make_async_copy(entries, places, sem.at[0])
     fetch.start()
 
@@ -297,7 +323,7 @@
 
     def edges(i, _):
         for u in range(2):
-            for src, z0 in ((zlo, 0), (zhi, HALO + Z_DEV)):
+            for src, z0 in ((z_outer, high * odd_slab), (z_inner, high * (1 - odd_slab))):
                 zi = i * 2 + u
                 for j in range(Y_DEV // 2):
                     a = src[zi, 2 * j // 8, pl.ds(2 * j % 8, 8, stride=8), :]
@@ -331,7 +357,7 @@
 
     lax.fori_loop(0, EXT // 4, first_sums, 0)
     fetch.wait()
-    count = prepare_points(((points, 0),), tiles, prep, places, todo)
+    count = prepare_points(((points, 0),), tiles, 8, prep, places, todo)
     splat_slots(count, todo, prep, stage, accd, accr)
 
 
@@ -344,8 +370,9 @@
     pays = ((pay_outer, base), (pay_inner, base))
     at_zlo, at_zhi, at_ylo, at_yhi, odd = (flags[k] for k in range(5))
     side = 2 * odd - 1
-    find_places(pay_outer, base, tiles, 0, side, entries)
-    find_places(pay_inner, base, tiles, 1, -side, entries)
+    last = pl.ds(base + tiles * 6, 8)
+    find_places(pay_outer[last, :], tiles, 0, side, entries)
+    find_places(pay_inner[last, :], tiles, 1, -side, entries)
     high = (HALO + Y_DEV) // 2
     fetch = pltpu.make_async_copy(entries, places, sem.at[0])
     fetch.start()
@@ -369,7 +396,7 @@
 
     lax.fori_loop(0, HALO // 2, corners, 0)
     fetch.wait()
-    count = prepare_points(pays, tiles, prep, places, todo)
+    count = prepare_points(pays, tiles, 6, prep, places, todo)
     splat_slots(count, todo, prep, stage, accd, accr)
 
     def finish(i, _):
@@ -484,11 +511,12 @@
         leave(z).wait()
 
 
-def corner_kernel(odd_ref, zlo, zhi, points, outer, inner):
-    odd = odd_ref[0]
+def corner_kernel(z_outer, z_inner, points, outer, inner):
+    odd = lax.axis_index("row") % 2
+    odd_slab = lax.axis_index("slab") % 2
     ends = [(Y_DEV // 8 - 1) * side for side in (odd, 1 - odd)]
     starts = [(8 - HALO) * side for side in (odd, 1 - odd)]
-    for half, src in enumerate((zlo, zhi)):
+    for half, src in ((odd_slab, z_outer), (1 - odd_slab, z_inner)):
         def corner(z, _, half=half, src=src):
             for y in range(HALO):
                 at = pl.ds(((half * HALO + z) * HALO + y) * SUB, SUB)
@@ -498,15 +526,20 @@
 
         lax.fori_loop(0, HALO, corner, 0)
     base = 2 * HALO * HALO * SUB
+    tiles = points.shape[0] // 8
 
     def copy(i, _):
         for u in range(8):
-            block = points[pl.ds(i * 64 + u * 8, 8), :]
-            outer[pl.ds(base + i * 64 + u * 8, 8), :] = block
-            inner[pl.ds(base + i * 64 + u * 8, 8), :] = block
-        return 0
-
-    lax.fori_loop(0, points.shape[0] // 64, copy, 0)
+            block = points[pl.ds((i * 8 + u) * 8, 8), :]
+            at = pl.ds(base + (i * 8 + u) * 6, 8)
+            outer[at, :] = block
+            inner[at, :] = block
+        return 0
+
+    lax.fori_loop(0, tiles // 8, copy, 0)
+    bricks = brick_rows(points, tiles)
+    outer[pl.ds(base + tiles * 6, 8), :] = bricks
+    inner[pl.ds(base + tiles * 6, 8), :] = bricks
 
 
 def as_tiles(a):
@@ -527,25 +560,18 @@
     small = pltpu.CompilerParams(vmem_limit_bytes=8 * 1024 * 1024)
     split = as_tiles(guess)
     planes = jax.ShapeDtypeStruct((HALO,) + split.shape[1:], F32)
-    send, low_planes, high_planes = pl.pallas_call(
-        functools.partial(deal_kernel, n_row),
-        out_shape=(jax.ShapeDtypeStruct((peers, 3, 8, LANES), F32), planes, planes),
-        in_specs=[hbm] * 7,
-        out_specs=[vmem] * 3,
+    outer, inner = pl.pallas_call(
+        slab_kernel,
+        out_shape=(planes, planes),
+        in_specs=[hbm],
+        out_specs=[hbm] * 2,
         scratch_shapes=[
-            pltpu.SMEM((S_PEER, peers), jnp.int32),
-            pltpu.SMEM((S_PEER, peers), jnp.int32),
-            pltpu.VMEM((peers, S_PEER, CAP), jnp.int32),
-            pltpu.VMEM((peers, S_PEER, CAP), F32),
-            pltpu.VMEM((peers, 3, S_PEER, CAP), F32),
-            pltpu.VMEM((peers, S_PEER, CAP), F32),
-            pltpu.SemaphoreType.DMA((8,)),
+            pltpu.VMEM((4, HALO // 2) + split.shape[1:], F32),
+            pltpu.SemaphoreType.DMA((4,)),
+            pltpu.SemaphoreType.DMA((4,)),
         ],
-        compiler_params=pltpu.CompilerParams(vmem_limit_bytes=60 * 1024 * 1024),
-    )(
-        slot_brick[0].T, slot_count[0].T, split, point_cell[0], point_frac[0],
-        jnp.transpose(point_normal[0], (0, 2, 1, 3)), point_weight[0],
-    )
+        compiler_params=small,
+    )(pltpu.with_memory_space_constraint(split, pltpu.HBM))
 
     cells = RIM * RIM
     state = (
@@ -555,32 +581,51 @@
         jax.ShapeDtypeStruct(((EXT * PAIRS * 9 + 8 + 71) // 72 * 72, LANES), F32),
         jax.ShapeDtypeStruct((EXT * PAIRS, SUB, LANES), F32),
     )
-    zlo = lax.ppermute(high_planes, "slab", chain("slab", 1))
-    zhi = lax.ppermute(low_planes, "slab", chain("slab", -1))
+    z_outer = lax.ppermute(outer, "slab", swaps("slab", 1))
+    z_inner = lax.ppermute(inner, "slab", swaps("slab", 0))
+    send = pl.pallas_call(
+        functools.partial(deal_kernel, n_row),
+        out_shape=jax.ShapeDtypeStruct((peers, 3, 8, LANES), F32),
+        in_specs=[hbm] * 6,
+        out_specs=vmem,
+        scratch_shapes=[
+            pltpu.SMEM((S_PEER, peers), jnp.int32),
+            pltpu.SMEM((S_PEER, peers), jnp.int32),
+            pltpu.VMEM((peers, S_PEER, CAP), jnp.int32),
+            pltpu.VMEM((peers, S_PEER, CAP), F32),
+            pltpu.VMEM((peers, 3, S_PEER, CAP), F32),
+            pltpu.VMEM((peers, S_PEER, CAP), F32),
+            pltpu.SemaphoreType.DMA((6,)),
+        ],
+        compiler_params=small,
+    )(*(pltpu.with_memory_space_constraint(a, pltpu.HBM) for a in (
+        slot_brick[0].T, slot_count[0].T, point_cell[0], point_frac[0],
+        jnp.transpose(point_normal[0], (0, 2, 1, 3)), point_weight[0],
+    )))
     got = lax.all_to_all(send, ("slab", "row"), split_axis=0, concat_axis=0, tiled=True)
     ylo = lax.ppermute(split[:, -1], "row", chain("row", 1))
     yhi = lax.ppermute(split[:, 0], "row", chain("row", -1))
     points = got.reshape(tiles * 8, LANES)
 
     packed = pltpu.VMEM((EXT * PAIRS, SUB, LANES), F32)
-    pay = jax.ShapeDtypeStruct((2 * HALO * HALO * SUB + tiles * 8, LANES), F32)
+    pay = jax.ShapeDtypeStruct((2 * HALO * HALO * SUB + tiles * 6 + 8, LANES), F32)
     zi, yi = lax.axis_index("slab"), lax.axis_index("row")
     flags = jnp.stack([zi > 0, zi < n_slab - 1, yi > 0, yi < n_row - 1, yi % 2 == 1]).astype(jnp.int32)
-    outer, inner = pl.pallas_call(
+    row_outer, row_inner = pl.pallas_call(
         corner_kernel,
         out_shape=(pay, pay),
-        in_specs=[smem] + [vmem] * 3,
+        in_specs=[vmem] * 3,
         out_specs=[vmem] * 2,
         compiler_params=small,
-    )(flags[4:], zlo, zhi, points)
-    pay_outer = lax.ppermute(outer, "row", swaps("row", 1))
-    pay_inner = lax.ppermute(inner, "row", swaps("row", 0))
+    )(z_outer, z_inner, points)
+    pay_outer = lax.ppermute(row_outer, "row", swaps("row", 1))
+    pay_inner = lax.ppermute(row_inner, "row", swaps("row", 0))
 
     def lists(blocks):
         return [
             pltpu.SMEM((blocks * slots + 2 * UNROLL,), jnp.int32),
-            pltpu.VMEM((blocks * tiles, LANES), jnp.int32),
-            pltpu.SMEM((blocks * tiles, LANES), jnp.int32),
+            pltpu.VMEM((blocks * 8, LANES), jnp.int32),
+            pltpu.SMEM((blocks * 8, LANES), jnp.int32),
             pltpu.SemaphoreType.DMA((1,)),
         ]
 
@@ -598,7 +643,7 @@
         ] + lists(1),
         cost_estimate=pl.CostEstimate(flops=40_000_000_000, bytes_accessed=1_000_000, transcendentals=0),
         compiler_params=pltpu.CompilerParams(vmem_limit_bytes=limit(1, 6)),
-    )(split, zlo, zhi, ylo, yhi, points)
+    )(split, z_outer, z_inner, ylo, yhi, points)
     out = pl.pallas_call(
         functools.partial(relax_kernel, tiles),
         out_shape=state + (jax.ShapeDtypeStruct((Z_DEV, Y_DEV // 8, 8 * SUB, LANES), F32),),

time: 68 us -> 65.9 us (0.969)
  waiting for transfers between devices: 17.4 us -> 19.5 us
  starting transfers between devices: 20.2 us -> 18.2 us
  Pallas kernels: 27.7 us -> 25.9 us
    pallas_call x1, Pallas kernels: 16.1 us -> 13.6 us  [shards(): pl.pallas_call(functools.partial(relax_kernel, tiles), out_shape=state +...]
    ppermute x4, waiting for transfers between devices: 17.4 us -> 19.5 us  [the longest x1 9.13 us: shards(): z_outer = lax.ppermute(outer, 'slab', swaps('slab', 1))]
    ppermute x4, starting transfers between devices: 8.31 us -> 6.33 us  [the longest x1 3.09 us: shards(): z_outer = lax.ppermute(outer, 'slab', swaps('slab', 1))]
    pallas_call x2 -> x3, Pallas kernels: 3.69 us -> 4.78 us  [the longest x1 2.57 us: shards(): pl.pallas_call(functools.partial(deal_kernel, n_row), out_shape=jax.Shape...]
  transfers between devices with their start and end apart: 7 -> 7, of which waited for: 3 -> 3; matrix products, arithmetic and copies ran while one was open for 3% -> 2% of each run, Pallas kernels for 13% -> 15%
where the time goes in v3:
time: 65.9 us; the launch traced here: 65 us
  Pallas kernels  25.9 us (39%)
  waiting for transfers between devices  19.5 us (30%)
  starting transfers between devices  18.2 us (28%)
  local copies, waits for them, and re-layouts  1.26 us (2%)
    pallas_call x1, Pallas kernels, shards(): pl.pallas_call(functools.partial(relax_kernel, tiles), out_shape=state +...  13.6 us
    ppermute x1, waiting for transfers between devices, shards(): z_outer = lax.ppermute(outer, 'slab', swaps('slab', 1))  9.13 us
    ppermute x1, waiting for transfers between devices, shards(): z_inner = lax.ppermute(inner, 'slab', swaps('slab', 0))  8.62 us
    pallas_call x1, Pallas kernels, shards(): pl.pallas_call(functools.partial(near_kernel, tiles), out_shape=state, in...  7.48 us
    all_to_all x1, starting transfers between devices, shards(): lax.all_to_all(send, ('slab', 'row'), split_axis=0, concat_axis=0, tiled=...  6.33 us
    ppermute x1, starting transfers between devices, shards(): ylo = lax.ppermute(split[:, -1], 'row', chain('row', 1))  3.26 us
    ppermute x1, starting transfers between devices, shards(): z_outer = lax.ppermute(outer, 'slab', swaps('slab', 1))  3.09 us
    pallas_call x1, Pallas kernels, shards(): pl.pallas_call(functools.partial(deal_kernel, n_row), out_shape=jax.Shape...  2.57 us
  transfers between devices with their start and end apart: 7, of which 3 were waited for; matrix products, arithmetic and copies ran while one was open for 2% of the time, Pallas kernels for 15%

profile of v3, /device:TPU:9, one launch (start us, length us, event | category | flops | bytes accessed | tf_op | source)
XLA Modules:
  0.0 65.0 jit_solution(10328248888760679795)
XLA Ops:
  0.0 0.0 copy-start
  0.0 2.6 %shard_map.74 = f32[32,3,8,128]{3,2,1,0:T(8,128)} custom-call(s32[2,32]{1,0:T(2,128)} %bitcast.44, s32[2,32]{1,0:T(2,128)} %bitcast.45, s32[32,2,64]{2,1,0:T(2,128)} %bitcast.41, f32[32,2,64]{2,1,0:T(2,128)} %bitcast.42, f32[32,3,2,64]{3,2,1,0:T(2,128)} %bitcast.40, f32[32,2,64]{2,1,0:T(2,128)} %bitcast.43), custom_call_target="tpu_custom_call" | custom-call | tf_op jit(solution)/shard_map/pallas_call | solution.py:586
  2.6 6.3 %all-to-all-start = ((f32[32,3,8,128]{3,2,1,0:T(8,128)}), f32[32,3,8,128]{3,2,1,0:T(8,128)S(1)}, u32[]{:S(2)}, u32[]{:S(2)}) async-start(f32[32,3,8,128]{3,2,1,0:T(8,128)} %shard_map.74), calls=%async_computation | async-start | bytes 786432 | tf_op jit(solution)/shard_map/all_to_all | solution.py:605
  8.9 0.0 copy-done
  8.9 0.1 copy_bitcast_fusion
  9.0 0.0 copy-start.1
  9.0 1.1 %slice_bitcast_fusion = (f32[16,64,128]{2,1,0:T(8,128)}, f32[16,64,128]{2,1,0:T(8,128)}) fusion(f32[16,2,64,128]{3,2,0,1:T(8,128)S(1)} %copy_bitcast_fusion), kind=kLoop, calls=%fused_computation.1 | loop fusion | bytes 2097152 | tf_op jit(solution)/shard_map/squeeze | solution.py:607
  10.1 2.3 %collective-permute-start.5 = (f32[16,64,128]{2,1,0:T(8,128)}, f32[16,64,128]{2,1,0:T(8,128)S(1)}, u32[]{:S(2)}, u32[]{:S(2)}) collective-permute-start(f32[16,64,128]{2,1,0:T(8,128)} %get-tuple-element.25), channel_id=1, source_target_pairs={{1,0},{2,1},{3,2},{5,4},{6,5},{7,6},{9,8},{10,9},{11,10},{13,12},{... | collective-permute-start | bytes 1572872 | tf_op jit(solution)/shard_map/ppermute | solution.py:607
  12.4 3.3 %collective-permute-start.4 = (f32[16,64,128]{2,1,0:T(8,128)}, f32[16,64,128]{2,1,0:T(8,128)S(1)}, u32[]{:S(2)}, u32[]{:S(2)}) collective-permute-start(f32[16,64,128]{2,1,0:T(8,128)} %get-tuple-element.26), channel_id=1, source_target_pairs={{0,1},{1,2},{2,3},{4,5},{5,6},{6,7},{8,9},{9,10},{10,11},{12,13},{... | collective-permute-start | bytes 1572872 | tf_op jit(solution)/shard_map/ppermute | solution.py:606
  15.7 2.0 %shard_map.73 = (f32[6,2,64,128]{3,2,1,0:T(8,128)}, f32[6,2,64,128]{3,2,1,0:T(8,128)}) custom-call(f32[16,2,64,128]{3,2,1,0:T(8,128)} %bitcast.36), custom_call_target="tpu_custom_call" | custom-call | tf_op jit(solution)/shard_map/pallas_call | solution.py:563
  17.6 3.1 %collective-permute-start = (f32[6,2,64,128]{3,2,1,0:T(8,128)}, f32[6,2,64,128]{3,2,1,0:T(8,128)S(1)}, u32[]{:S(2)}, u32[]{:S(2)}) collective-permute-start(f32[6,2,64,128]{3,2,1,0:T(8,128)} %get-tuple-element.15), channel_id=1, source_target_pairs={{4,8},{12,16},{20,24},{8,4},{16,12},{24,20},{5,9},{13,17},{21,25},... | collective-permute-start | bytes 1179656 | tf_op jit(solution)/shard_map/ppermute | solution.py:584
  20.7 1.3 %collective-permute-start.1 = (f32[6,2,64,128]{3,2,1,0:T(8,128)}, f32[6,2,64,128]{3,2,1,0:T(8,128)S(1)}, u32[]{:S(2)}, u32[]{:S(2)}) collective-permute-start(f32[6,2,64,128]{3,2,1,0:T(8,128)} %get-tuple-element.16), channel_id=1, source_target_pairs={{0,4},{8,12},{16,20},{24,28},{4,0},{12,8},{20,16},{28,24},{1,5},{9... | collective-permute-start | bytes 1179656 | tf_op jit(solution)/shard_map/ppermute | solution.py:585
  22.0 0.1 stack.23
  22.1 9.1 %collective-permute-done.z_outer = f32[6,2,64,128]{3,2,1,0:T(8,128)S(1)} collective-permute-done((f32[6,2,64,128]{3,2,1,0:T(8,128)}, f32[6,2,64,128]{3,2,1,0:T(8,128)S(1)}, u32[]{:S(2)}, u32[]{:S(2)}) %collective-permute-start) | collective-permute-done | bytes 393248 | tf_op jit(solution)/shard_map/ppermute | solution.py:584
  31.2 8.6 %collective-permute-done.1.z_inner = f32[6,2,64,128]{3,2,1,0:T(8,128)S(1)} collective-permute-done((f32[6,2,64,128]{3,2,1,0:T(8,128)}, f32[6,2,64,128]{3,2,1,0:T(8,128)S(1)}, u32[]{:S(2)}, u32[]{:S(2)}) %collective-permute-start.1) | collective-permute-done | bytes 393248 | tf_op jit(solution)/shard_map/ppermute | solution.py:585
  39.8 0.0 all-to-all-done
  39.8 0.2 shard_map.75
  40.1 1.9 %collective-permute-start.2 = (f32[1160,128]{1,0:T(8,128)S(1)}, f32[1160,128]{1,0:T(8,128)S(1)}, u32[]{:S(2)}, u32[]{:S(2)}) collective-permute-start(f32[1160,128]{1,0:T(8,128)S(1)} %get-tuple-element.17), channel_id=1, source_target_pairs={{1,2},{2,1},{5,6},{6,5},{9,10},{10,9},{13,14},{14,13},{17,18},{18,... | collective-permute-start | bytes 1781768 | tf_op jit(solution)/shard_map/ppermute | solution.py:621
  42.0 0.1 collective-permute-start.3
  42.1 0.0 collective-permute-done.5.yhi
  42.1 0.0 collective-permute-done.4.ylo
  42.1 0.0 copy-done.1
  42.1 7.5 %shard_map.76 = (f32[900,8,128]{2,1,0:T(8,128)S(1)}, f32[900,8,128]{2,1,0:T(8,128)S(1)}, f32[3600,128]{1,0:T(8,128)S(1)}, f32[3600,128]{1,0:T(8,128)S(1)}, f32[392,8,128]{2,1,0:T(8,128)S(1)}) custom-call(f32[16,2,64,128]{3,2,1,0:T(8,128)S(1)} %bitcast.37, f32[6,2,64,128]{3,2,1,0:T(8,128)S(1)} %collective-permute-done.z_outer, ...), custom_call_target="tpu_custom_call" | custom-call | flops 40000000000 | bytes 1000000 | tf_op jit(solution)/shard_map/pallas_call | solution.py:635
  49.6 1.7 %collective-permute-done.2.pay_outer = f32[1160,128]{1,0:T(8,128)S(1)} collective-permute-done((f32[1160,128]{1,0:T(8,128)S(1)}, f32[1160,128]{1,0:T(8,128)S(1)}, u32[]{:S(2)}, u32[]{:S(2)}) %collective-permute-start.2) | collective-permute-done | bytes 593952 | tf_op jit(solution)/shard_map/ppermute | solution.py:621
  51.3 0.0 collective-permute-done.3.pay_inner
  51.3 13.6 %shard_map.77 = (f32[900,8,128]{2,1,0:T(8,128)S(1)}, f32[900,8,128]{2,1,0:T(8,128)S(1)}, f32[3600,128]{1,0:T(8,128)S(1)}, f32[3600,128]{1,0:T(8,128)S(1)}, f32[3...) custom-call(s32[5]{0:T(128)S(1)} %convert_element_type.3.flags, ...), custom_call_target="tpu_custom_call", output_to_operand_aliasing={{0}: (3, {}), {1}: (4, {}), {2}: (5, {}), {3}: (6, {}), {4}... | custom-call | tf_op jit(solution)/shard_map/pallas_call | solution.py:647
  (1 shorter events, 0.0 us)
Async XLA Ops:
  0.0 8.9 %copy-start = (f32[16,16,1024]{2,1,0:T(8,128)S(1)}, f32[16,16,1024]{2,1,0:T(8,128)}, u32[]{:S(2)}) copy-start(f32[16,16,1024]{2,1,0:T(8,128)} %param.13) | copy-start | bytes 3145732
  2.6 37.3 %all-to-all-start = ((f32[32,3,8,128]{3,2,1,0:T(8,128)}), f32[32,3,8,128]{3,2,1,0:T(8,128)S(1)}, u32[]{:S(2)}, u32[]{:S(2)}) async-start(f32[32,3,8,128]{3,2,1,0:T(8,128)} %shard_map.74), calls=%async_computation | async-start | bytes 786432 | tf_op jit(solution)/shard_map/all_to_all | solution.py:605
  9.0 33.1 %copy-start.1 = (f32[16,16,1024]{2,1,0:T(8,128)S(1)}, f32[16,16,1024]{2,1,0:T(8,128)}, u32[]{:S(2)}) copy-start(f32[16,16,1024]{2,1,0:T(8,128)} %param.13) | copy-start | bytes 3145732
  10.1 32.0 %collective-permute-start.5 = (f32[16,64,128]{2,1,0:T(8,128)}, f32[16,64,128]{2,1,0:T(8,128)S(1)}, u32[]{:S(2)}, u32[]{:S(2)}) collective-permute-start(f32[16,64,128]{2,1,0:T(8,128)} %get-tuple-element.25), channel_id=1, source_target_pairs={{1,0},{2,1},{3,2},{5,4},{6,5},{7,6},{9,8},{10,9},{11,10},{13,12},{... | collective-permute-start | bytes 1572872 | tf_op jit(solution)/shard_map/ppermute | solution.py:607
  12.4 29.7 %collective-permute-start.4 = (f32[16,64,128]{2,1,0:T(8,128)}, f32[16,64,128]{2,1,0:T(8,128)S(1)}, u32[]{:S(2)}, u32[]{:S(2)}) collective-permute-start(f32[16,64,128]{2,1,0:T(8,128)} %get-tuple-element.26), channel_id=1, source_target_pairs={{0,1},{1,2},{2,3},{4,5},{5,6},{6,7},{8,9},{9,10},{10,11},{12,13},{... | collective-permute-start | bytes 1572872 | tf_op jit(solution)/shard_map/ppermute | solution.py:606
  17.6 13.6 %collective-permute-start = (f32[6,2,64,128]{3,2,1,0:T(8,128)}, f32[6,2,64,128]{3,2,1,0:T(8,128)S(1)}, u32[]{:S(2)}, u32[]{:S(2)}) collective-permute-start(f32[6,2,64,128]{3,2,1,0:T(8,128)} %get-tuple-element.15), channel_id=1, source_target_pairs={{4,8},{12,16},{20,24},{8,4},{16,12},{24,20},{5,9},{13,17},{21,25},... | collective-permute-start | bytes 1179656 | tf_op jit(solution)/shard_map/ppermute | solution.py:584
  20.7 19.1 %collective-permute-start.1 = (f32[6,2,64,128]{3,2,1,0:T(8,128)}, f32[6,2,64,128]{3,2,1,0:T(8,128)S(1)}, u32[]{:S(2)}, u32[]{:S(2)}) collective-permute-start(f32[6,2,64,128]{3,2,1,0:T(8,128)} %get-tuple-element.16), channel_id=1, source_target_pairs={{0,4},{8,12},{16,20},{24,28},{4,0},{12,8},{20,16},{28,24},{1,5},{9... | collective-permute-start | bytes 1179656 | tf_op jit(solution)/shard_map/ppermute | solution.py:585
  40.1 11.2 %collective-permute-start.2 = (f32[1160,128]{1,0:T(8,128)S(1)}, f32[1160,128]{1,0:T(8,128)S(1)}, u32[]{:S(2)}, u32[]{:S(2)}) collective-permute-start(f32[1160,128]{1,0:T(8,128)S(1)} %get-tuple-element.17), channel_id=1, source_target_pairs={{1,2},{2,1},{5,6},{6,5},{9,10},{10,9},{13,14},{14,13},{17,18},{18,... | collective-permute-start | bytes 1781768 | tf_op jit(solution)/shard_map/ppermute | solution.py:621
  42.0 9.3 %collective-permute-start.3 = (f32[1160,128]{1,0:T(8,128)S(1)}, f32[1160,128]{1,0:T(8,128)S(1)}, u32[]{:S(2)}, u32[]{:S(2)}) collective-permute-start(f32[1160,128]{1,0:T(8,128)S(1)} %get-tuple-element.18), channel_id=1, source_target_pairs={{0,1},{2,3},{1,0},{3,2},{4,5},{6,7},{5,4},{7,6},{8,9},{10,11},{9,8... | collective-permute-start | bytes 1781768 | tf_op jit(solution)/shard_map/ppermute | solution.py:622

commit v4 on v3

--- a/solution.py
+++ b/solution.py
@@ -22,6 +22,7 @@
 SUB = NX // LANES
 CODE = 16384
 UNROLL = 16
+STRIDE = 12
 F32 = jnp.float32
 BF16 = jnp.bfloat16
 
@@ -472,32 +473,26 @@
             keep(k, first + 2 + u, ahead[u])
         steps = (EXT - 2 * k) // 2
 
-        def body(p, k=k, first=first, n=2):
-            ahead = [sides(k, p + n + u) for u in range(n)]
-            for u in range(n):
-                advance(k, p + u, first + u, True, True)
-            for u in range(n):
-                keep(k, p + n + u, ahead[u])
-
-        def body4(i, _, k=k, first=first, body=body):
-            p = first + 2 + i * 4
-            ahead = [sides(k, p + 2 + u) for u in range(4)]
-            advance(k, p, first, True, True)
-            advance(k, p + 1, first + 1, True, True)
-            for u in range(4):
-                keep(k, p + 2 + u, ahead[u])
-            advance(k, p + 2, first, True, True)
-            advance(k, p + 3, first + 1, True, True)
-            if k == HALO:
-                unpack(i * 4)
-                unpack(i * 4 + 2)
+        def body(p, count, k=k, first=first):
+            for c in range(0, 2 * count, 2):
+                ahead = [sides(k, p + c + 2 + u) for u in range(2)]
+                advance(k, p + c, first, True, True)
+                advance(k, p + c + 1, first + 1, True, True)
+                for u in range(2):
+                    keep(k, p + c + 2 + u, ahead[u])
+                if k == HALO:
+                    unpack(p + c - first - 2)
+
+        loops, rest = divmod(steps - 1, STRIDE)
+        if rest:
+            body(first + 2, rest)
+
+        def run(i, _, k=k, start=first + 2 + 2 * rest, body=body):
+            body(start + i * (2 * STRIDE), STRIDE)
             return 0
 
-        lax.fori_loop(0, (steps - 1) // 2, body4, 0)
-        if (steps - 1) % 2:
-            body(first + 2 + (steps - 2) * 2)
-            if k == HALO:
-                unpack((steps - 2) * 2)
+        if loops:
+            lax.fori_loop(0, loops, run, 0)
         p = first + 2 * steps
         ahead = [sides(k + 1, k + u) for u in range(2)] if k < HALO else []
         advance(k, p, first, True, True)

time: 65.9 us -> 63.8 us (0.968)
  Pallas kernels: 25.9 us -> 23.8 us
    pallas_call x1, Pallas kernels: 13.6 us -> 11.5 us  [shards(): pl.pallas_call(functools.partial(relax_kernel, tiles), out_shape=state +...]
where the time goes in v4:
time: 63.8 us; the launch traced here: 62.9 us
  Pallas kernels  23.8 us (37%)
  waiting for transfers between devices  19.5 us (31%)
  starting transfers between devices  18.2 us (29%)
  local copies, waits for them, and re-layouts  1.26 us (2%)
    pallas_call x1, Pallas kernels, shards(): pl.pallas_call(functools.partial(relax_kernel, tiles), out_shape=state +...  11.5 us
    ppermute x1, waiting for transfers between devices, shards(): z_outer = lax.ppermute(outer, 'slab', swaps('slab', 1))  9.13 us
    ppermute x1, waiting for transfers between devices, shards(): z_inner = lax.ppermute(inner, 'slab', swaps('slab', 0))  8.62 us
    pallas_call x1, Pallas kernels, shards(): pl.pallas_call(functools.partial(near_kernel, tiles), out_shape=state, in...  7.48 us
    all_to_all x1, starting transfers between devices, shards(): lax.all_to_all(send, ('slab', 'row'), split_axis=0, concat_axis=0, tiled=...  6.33 us
    ppermute x1, starting transfers between devices, shards(): ylo = lax.ppermute(split[:, -1], 'row', chain('row', 1))  3.26 us
    ppermute x1, starting transfers between devices, shards(): z_outer = lax.ppermute(outer, 'slab', swaps('slab', 1))  3.09 us
    pallas_call x1, Pallas kernels, shards(): pl.pallas_call(functools.partial(deal_kernel, n_row), out_shape=jax.Shape...  2.57 us
  transfers between devices with their start and end apart: 7, of which 3 were waited for; matrix products, arithmetic and copies ran while one was open for 2% of the time, Pallas kernels for 15%

profile of v4, /device:TPU:9, one launch (start us, length us, event | category | flops | bytes accessed | tf_op | source)
XLA Modules:
  0.0 62.9 jit_solution(14438303088502578310)
XLA Ops:
  0.0 0.0 copy-start
  0.0 2.6 %shard_map.74 = f32[32,3,8,128]{3,2,1,0:T(8,128)} custom-call(s32[2,32]{1,0:T(2,128)} %bitcast.44, s32[2,32]{1,0:T(2,128)} %bitcast.45, s32[32,2,64]{2,1,0:T(2,128)} %bitcast.41, f32[32,2,64]{2,1,0:T(2,128)} %bitcast.42, f32[32,3,2,64]{3,2,1,0:T(2,128)} %bitcast.40, f32[32,2,64]{2,1,0:T(2,128)} %bitcast.43), custom_call_target="tpu_custom_call" | custom-call | tf_op jit(solution)/shard_map/pallas_call | solution.py:581
  2.6 6.3 %all-to-all-start = ((f32[32,3,8,128]{3,2,1,0:T(8,128)}), f32[32,3,8,128]{3,2,1,0:T(8,128)S(1)}, u32[]{:S(2)}, u32[]{:S(2)}) async-start(f32[32,3,8,128]{3,2,1,0:T(8,128)} %shard_map.74), calls=%async_computation | async-start | bytes 786432 | tf_op jit(solution)/shard_map/all_to_all | solution.py:600
  8.9 0.0 copy-done
  8.9 0.1 copy_bitcast_fusion
  9.0 0.0 copy-start.1
  9.0 1.1 %slice_bitcast_fusion = (f32[16,64,128]{2,1,0:T(8,128)}, f32[16,64,128]{2,1,0:T(8,128)}) fusion(f32[16,2,64,128]{3,2,0,1:T(8,128)S(1)} %copy_bitcast_fusion), kind=kLoop, calls=%fused_computation.1 | loop fusion | bytes 2097152 | tf_op jit(solution)/shard_map/squeeze | solution.py:602
  10.1 2.3 %collective-permute-start.5 = (f32[16,64,128]{2,1,0:T(8,128)}, f32[16,64,128]{2,1,0:T(8,128)S(1)}, u32[]{:S(2)}, u32[]{:S(2)}) collective-permute-start(f32[16,64,128]{2,1,0:T(8,128)} %get-tuple-element.25), channel_id=1, source_target_pairs={{1,0},{2,1},{3,2},{5,4},{6,5},{7,6},{9,8},{10,9},{11,10},{13,12},{... | collective-permute-start | bytes 1572872 | tf_op jit(solution)/shard_map/ppermute | solution.py:602
  12.4 3.3 %collective-permute-start.4 = (f32[16,64,128]{2,1,0:T(8,128)}, f32[16,64,128]{2,1,0:T(8,128)S(1)}, u32[]{:S(2)}, u32[]{:S(2)}) collective-permute-start(f32[16,64,128]{2,1,0:T(8,128)} %get-tuple-element.26), channel_id=1, source_target_pairs={{0,1},{1,2},{2,3},{4,5},{5,6},{6,7},{8,9},{9,10},{10,11},{12,13},{... | collective-permute-start | bytes 1572872 | tf_op jit(solution)/shard_map/ppermute | solution.py:601
  15.7 2.0 %shard_map.73 = (f32[6,2,64,128]{3,2,1,0:T(8,128)}, f32[6,2,64,128]{3,2,1,0:T(8,128)}) custom-call(f32[16,2,64,128]{3,2,1,0:T(8,128)} %bitcast.36), custom_call_target="tpu_custom_call" | custom-call | tf_op jit(solution)/shard_map/pallas_call | solution.py:558
  17.6 3.1 %collective-permute-start = (f32[6,2,64,128]{3,2,1,0:T(8,128)}, f32[6,2,64,128]{3,2,1,0:T(8,128)S(1)}, u32[]{:S(2)}, u32[]{:S(2)}) collective-permute-start(f32[6,2,64,128]{3,2,1,0:T(8,128)} %get-tuple-element.15), channel_id=1, source_target_pairs={{4,8},{12,16},{20,24},{8,4},{16,12},{24,20},{5,9},{13,17},{21,25},... | collective-permute-start | bytes 1179656 | tf_op jit(solution)/shard_map/ppermute | solution.py:579
  20.7 1.3 %collective-permute-start.1 = (f32[6,2,64,128]{3,2,1,0:T(8,128)}, f32[6,2,64,128]{3,2,1,0:T(8,128)S(1)}, u32[]{:S(2)}, u32[]{:S(2)}) collective-permute-start(f32[6,2,64,128]{3,2,1,0:T(8,128)} %get-tuple-element.16), channel_id=1, source_target_pairs={{0,4},{8,12},{16,20},{24,28},{4,0},{12,8},{20,16},{28,24},{1,5},{9... | collective-permute-start | bytes 1179656 | tf_op jit(solution)/shard_map/ppermute | solution.py:580
  22.0 0.1 stack.23
  22.1 9.1 %collective-permute-done.z_outer = f32[6,2,64,128]{3,2,1,0:T(8,128)S(1)} collective-permute-done((f32[6,2,64,128]{3,2,1,0:T(8,128)}, f32[6,2,64,128]{3,2,1,0:T(8,128)S(1)}, u32[]{:S(2)}, u32[]{:S(2)}) %collective-permute-start) | collective-permute-done | bytes 393248 | tf_op jit(solution)/shard_map/ppermute | solution.py:579
  31.2 8.6 %collective-permute-done.1.z_inner = f32[6,2,64,128]{3,2,1,0:T(8,128)S(1)} collective-permute-done((f32[6,2,64,128]{3,2,1,0:T(8,128)}, f32[6,2,64,128]{3,2,1,0:T(8,128)S(1)}, u32[]{:S(2)}, u32[]{:S(2)}) %collective-permute-start.1) | collective-permute-done | bytes 393248 | tf_op jit(solution)/shard_map/ppermute | solution.py:580
  39.8 0.0 all-to-all-done
  39.8 0.2 shard_map.75
  40.1 1.9 %collective-permute-start.2 = (f32[1160,128]{1,0:T(8,128)S(1)}, f32[1160,128]{1,0:T(8,128)S(1)}, u32[]{:S(2)}, u32[]{:S(2)}) collective-permute-start(f32[1160,128]{1,0:T(8,128)S(1)} %get-tuple-element.17), channel_id=1, source_target_pairs={{1,2},{2,1},{5,6},{6,5},{9,10},{10,9},{13,14},{14,13},{17,18},{18,... | collective-permute-start | bytes 1781768 | tf_op jit(solution)/shard_map/ppermute | solution.py:616
  42.0 0.1 collective-permute-start.3
  42.1 0.0 collective-permute-done.5.yhi
  42.1 0.0 collective-permute-done.4.ylo
  42.1 0.0 copy-done.1
  42.1 7.5 %shard_map.76 = (f32[900,8,128]{2,1,0:T(8,128)S(1)}, f32[900,8,128]{2,1,0:T(8,128)S(1)}, f32[3600,128]{1,0:T(8,128)S(1)}, f32[3600,128]{1,0:T(8,128)S(1)}, f32[392,8,128]{2,1,0:T(8,128)S(1)}) custom-call(f32[16,2,64,128]{3,2,1,0:T(8,128)S(1)} %bitcast.37, f32[6,2,64,128]{3,2,1,0:T(8,128)S(1)} %collective-permute-done.z_outer, ...), custom_call_target="tpu_custom_call" | custom-call | flops 40000000000 | bytes 1000000 | tf_op jit(solution)/shard_map/pallas_call | solution.py:630
  49.6 1.7 %collective-permute-done.2.pay_outer = f32[1160,128]{1,0:T(8,128)S(1)} collective-permute-done((f32[1160,128]{1,0:T(8,128)S(1)}, f32[1160,128]{1,0:T(8,128)S(1)}, u32[]{:S(2)}, u32[]{:S(2)}) %collective-permute-start.2) | collective-permute-done | bytes 593952 | tf_op jit(solution)/shard_map/ppermute | solution.py:616
  51.3 0.0 collective-permute-done.3.pay_inner
  51.3 11.5 %shard_map.77 = (f32[900,8,128]{2,1,0:T(8,128)S(1)}, f32[900,8,128]{2,1,0:T(8,128)S(1)}, f32[3600,128]{1,0:T(8,128)S(1)}, f32[3600,128]{1,0:T(8,128)S(1)}, f32[3...) custom-call(s32[5]{0:T(128)S(1)} %convert_element_type.3.flags, ...), custom_call_target="tpu_custom_call", output_to_operand_aliasing={{0}: (3, {}), {1}: (4, {}), {2}: (5, {}), {3}: (6, {}), {4}... | custom-call | tf_op jit(solution)/shard_map/pallas_call | solution.py:642
  (1 shorter events, 0.0 us)
Async XLA Ops:
  0.0 8.9 %copy-start = (f32[16,16,1024]{2,1,0:T(8,128)S(1)}, f32[16,16,1024]{2,1,0:T(8,128)}, u32[]{:S(2)}) copy-start(f32[16,16,1024]{2,1,0:T(8,128)} %param.13) | copy-start | bytes 3145732
  2.6 37.3 %all-to-all-start = ((f32[32,3,8,128]{3,2,1,0:T(8,128)}), f32[32,3,8,128]{3,2,1,0:T(8,128)S(1)}, u32[]{:S(2)}, u32[]{:S(2)}) async-start(f32[32,3,8,128]{3,2,1,0:T(8,128)} %shard_map.74), calls=%async_computation | async-start | bytes 786432 | tf_op jit(solution)/shard_map/all_to_all | solution.py:600
  9.0 33.1 %copy-start.1 = (f32[16,16,1024]{2,1,0:T(8,128)S(1)}, f32[16,16,1024]{2,1,0:T(8,128)}, u32[]{:S(2)}) copy-start(f32[16,16,1024]{2,1,0:T(8,128)} %param.13) | copy-start | bytes 3145732
  10.1 32.0 %collective-permute-start.5 = (f32[16,64,128]{2,1,0:T(8,128)}, f32[16,64,128]{2,1,0:T(8,128)S(1)}, u32[]{:S(2)}, u32[]{:S(2)}) collective-permute-start(f32[16,64,128]{2,1,0:T(8,128)} %get-tuple-element.25), channel_id=1, source_target_pairs={{1,0},{2,1},{3,2},{5,4},{6,5},{7,6},{9,8},{10,9},{11,10},{13,12},{... | collective-permute-start | bytes 1572872 | tf_op jit(solution)/shard_map/ppermute | solution.py:602
  12.4 29.7 %collective-permute-start.4 = (f32[16,64,128]{2,1,0:T(8,128)}, f32[16,64,128]{2,1,0:T(8,128)S(1)}, u32[]{:S(2)}, u32[]{:S(2)}) collective-permute-start(f32[16,64,128]{2,1,0:T(8,128)} %get-tuple-element.26), channel_id=1, source_target_pairs={{0,1},{1,2},{2,3},{4,5},{5,6},{6,7},{8,9},{9,10},{10,11},{12,13},{... | collective-permute-start | bytes 1572872 | tf_op jit(solution)/shard_map/ppermute | solution.py:601
  17.6 13.6 %collective-permute-start = (f32[6,2,64,128]{3,2,1,0:T(8,128)}, f32[6,2,64,128]{3,2,1,0:T(8,128)S(1)}, u32[]{:S(2)}, u32[]{:S(2)}) collective-permute-start(f32[6,2,64,128]{3,2,1,0:T(8,128)} %get-tuple-element.15), channel_id=1, source_target_pairs={{4,8},{12,16},{20,24},{8,4},{16,12},{24,20},{5,9},{13,17},{21,25},... | collective-permute-start | bytes 1179656 | tf_op jit(solution)/shard_map/ppermute | solution.py:579
  20.7 19.1 %collective-permute-start.1 = (f32[6,2,64,128]{3,2,1,0:T(8,128)}, f32[6,2,64,128]{3,2,1,0:T(8,128)S(1)}, u32[]{:S(2)}, u32[]{:S(2)}) collective-permute-start(f32[6,2,64,128]{3,2,1,0:T(8,128)} %get-tuple-element.16), channel_id=1, source_target_pairs={{0,4},{8,12},{16,20},{24,28},{4,0},{12,8},{20,16},{28,24},{1,5},{9... | collective-permute-start | bytes 1179656 | tf_op jit(solution)/shard_map/ppermute | solution.py:580
  40.1 11.2 %collective-permute-start.2 = (f32[1160,128]{1,0:T(8,128)S(1)}, f32[1160,128]{1,0:T(8,128)S(1)}, u32[]{:S(2)}, u32[]{:S(2)}) collective-permute-start(f32[1160,128]{1,0:T(8,128)S(1)} %get-tuple-element.17), channel_id=1, source_target_pairs={{1,2},{2,1},{5,6},{6,5},{9,10},{10,9},{13,14},{14,13},{17,18},{18,... | collective-permute-start | bytes 1781768 | tf_op jit(solution)/shard_map/ppermute | solution.py:616
  42.0 9.3 %collective-permute-start.3 = (f32[1160,128]{1,0:T(8,128)S(1)}, f32[1160,128]{1,0:T(8,128)S(1)}, u32[]{:S(2)}, u32[]{:S(2)}) collective-permute-start(f32[1160,128]{1,0:T(8,128)S(1)} %get-tuple-element.18), channel_id=1, source_target_pairs={{0,1},{2,3},{1,0},{3,2},{4,5},{6,7},{5,4},{7,6},{8,9},{10,11},{9,8... | collective-permute-start | bytes 1781768 | tf_op jit(solution)/shard_map/ppermute | solution.py:617
